TPU v7x, 32 devices: a whole 2x2x4 slice. The times are simulated.
32 devices in a mesh: blk: 16 (over z, y, core), rhs: 2 (over x).
Axes of the slice: x: 2, y: 2, z: 4, core: 2. Of those that a mesh axis runs over, the one named last changes fastest.
Arguments:
- signal: bfloat16 [131072, 256], P('blk', 'rhs'), may hold values from -6 to 6
- col_factor: bfloat16 [96, 131072], P(None, 'blk'), may hold values from -0.5 to 0.5
- row_factor: bfloat16 [96, 131072], P(None, 'blk'), may hold values from -0.625 to 0.625
- level_factor: bfloat16 [4, 16, 2, 64, 48, 192], P(None, 'blk', None, 'rhs'), may hold values from -0.4375 to 0.4375
- col_leaf_sizes: int32 [16, 128], P('blk'), may hold values from 1 to 128, 8192 in all within a row
- row_leaf_sizes: int32 [16, 128], P('blk'), may hold values from 1 to 128, 8192 in all within a row
- level_order: int32 [4, 16, 128], P(None, 'blk'), may hold values from 0 to 127, each once within a row
Outputs:
- result: bfloat16 [131072, 256], P('blk', 'rhs')
Inputs may be any that keep to these rules, and one draw needn't show every extreme that they name: `col_leaf_sizes`: row d lists in order the sizes of the 128 column leaves that cover unknowns d * 8192 to (d + 1) * 8192 - 1; each row sums to 8192 and its largest entry is 128. `row_leaf_sizes`: row d lists in order the sizes of the 128 row leaves that cover unknowns d * 8192 to (d + 1) * 8192 - 1; each row sums to 8192 and its largest entry is 128. Every level_order[l, d, :] is a permutation of 0 to 127.
All inputs are finite; a program needn't handle non-finite values.
Results may differ from a plain program's by a relative error of at most 0.0076.
Values may be sent and summed in bfloat16 or wider, within the bound.
No kernel may reach another device: no remote copies, remote signals or barrier semaphores. Data moves between devices by JAX's collectives and lax.ppermute only.
A program may use at most 128 MiB of HBM per device.

v0:
```python
import functools

import jax
import jax.numpy as jnp
from jax import lax
from jax.experimental import pallas as pl
from jax.experimental.pallas import tpu as pltpu
from jax.sharding import PartitionSpec as P


LEAFMAX = 128
LEAF_IN_KIB = 50300
SPLIT_KIB = 50000
TILE = 128
ROWS = 16

SMEM = pl.BlockSpec(memory_space=pltpu.SMEM)
VMEM = pl.BlockSpec(memory_space=pltpu.VMEM)
ANY = pl.BlockSpec(memory_space=pl.ANY)
HBM = pl.BlockSpec(memory_space=pltpu.HBM)


def cost(micros):
    return pl.CostEstimate(flops=micros * 10**7, bytes_accessed=0, transcendentals=0)


def sign_row(rows, columns):
    lane = lax.broadcasted_iota(jnp.int32, (rows, columns), 1)
    return jnp.where(lane < columns // 2, -1.0, 1.0)


def turned(values, sign):
    return pltpu.roll(values, values.shape[-1] // 2, 1) * sign


def place_starts(sizes_ref, starts_ref):
    def place(b, total):
        starts_ref[b] = total
        return total + sizes_ref[b]

    lax.fori_loop(0, sizes_ref.shape[0], place, jnp.int32(0), unroll=8)


def leaf_in_kernel(
    groups, leaves_ref, signal_hbm, factor_hbm, levels_hbm, out_ref, slots_ref, *refs
):
    count = levels_hbm.shape[0]
    first_ref, dense_ref, *refs = refs
    sizes_ref = leaves_ref.at[count]
    starts, signal, factor, inward, arrive = refs
    leaves, rank, columns = out_ref.shape
    points = signal.shape[0]
    early = leaves // 4
    pieces = 8
    rows = points // pieces
    first = -(-min(points, early * LEAFMAX + 2 * TILE) // rows)

    def pulled(source, target, at, sem):
        return pltpu.make_async_copy(source.at[at], target.at[at], inward.at[sem])

    by_rows = [pulled(signal_hbm, signal, pl.ds(k * rows, rows), k) for k in range(pieces)]
    by_ranks = [
        pulled(factor_hbm, factor, pl.ds(k * ROWS, ROWS), pieces + k)
        for k in range(2 * rank // ROWS)
    ]
    inputs = [by_ranks + by_rows[:first], by_rows[first:]]
    loads = [
        pltpu.make_async_copy(levels_hbm.at[0, :, h], first_ref.at[:, h], arrive.at[h])
        for h in range(first_ref.shape[1])
    ]
    for copy in inputs[0] + inputs[1]:
        copy.start()
    peer_blocks = leaves // groups
    me = lax.axis_index("blk")
    place_starts(sizes_ref, starts)

    def place_slot(j, carry):
        slot = ((j // peer_blocks) ^ me) * peer_blocks + j % peer_blocks
        for level in range(count):
            slots_ref[level, leaves_ref[level, j]] = slot
        return carry

    lax.fori_loop(0, leaves, place_slot, 0, unroll=8)
    lane = lax.broadcasted_iota(jnp.int32, (ROWS, 2 * TILE), 1)
    sign = sign_row(rank, columns)

    def body(leaf, carry):
        start = starts[leaf]
        chunk = jnp.minimum(start // TILE, points // TILE - 2)
        base = pl.multiple_of(chunk * TILE, TILE)
        low = start - base
        inside = (lane >= low) & (lane < low + sizes_ref[leaf])
        keep = jnp.where(inside, 1.0, 0.0).astype(jnp.bfloat16)
        weights = factor[:, pl.ds(base, 2 * TILE)]
        weights = weights.reshape(2 * rank // ROWS, ROWS, 2 * TILE) * keep[None]
        weights = weights.reshape(2 * rank, 2 * TILE)
        sums = jnp.dot(
            weights, signal[pl.ds(base, 2 * TILE), :], preferred_element_type=jnp.float32
        )
        value = sums[:rank] + turned(sums[rank:], sign)
        out_ref[slots_ref[0, leaf]] = value.astype(out_ref.dtype)
        return carry

    for copy in inputs[0]:
        copy.wait()
    for copy in loads:
        copy.start()
    lax.fori_loop(0, early, body, 0, unroll=32)
    for copy in inputs[1]:
        copy.wait()
    lax.fori_loop(early, leaves, body, 0, unroll=32)
    for copy in loads:
        copy.wait()
    width = first_ref.shape[2]

    def pack(i, carry):
        low, high = first_ref[0, 0, i], first_ref[0, 1, i]
        dense_ref[i] = low[:, :TILE]
        dense_ref[width + i] = high[:, :TILE]
        dense_ref[2 * width + i] = jnp.concatenate([low[:, TILE:], high[:, TILE:]], axis=1)
        return carry

    lax.fori_loop(0, width, pack, 0, unroll=8)


def leaf_in(sizes, order, signal, factor, level_factor, groups):
    _, columns = signal.shape
    leaves = sizes.shape[1]
    rank = factor.shape[0] // 2
    count = level_factor.shape[0]
    level = jax.ShapeDtypeStruct(level_factor.shape[1:], level_factor.dtype)
    return pl.pallas_call(
        functools.partial(leaf_in_kernel, groups),
        out_shape=[
            jax.ShapeDtypeStruct((leaves, rank, columns), jnp.bfloat16),
            jax.ShapeDtypeStruct((count, leaves), jnp.int32),
            level,
            jax.ShapeDtypeStruct((3 * level.shape[2], rank, TILE), level_factor.dtype),
        ],
        in_specs=[SMEM, HBM, HBM, HBM],
        out_specs=[VMEM, SMEM, VMEM, VMEM],
        scratch_shapes=[
            pltpu.SMEM((leaves,), jnp.int32),
            pltpu.VMEM(signal.shape, signal.dtype),
            pltpu.VMEM(factor.shape, factor.dtype),
            pltpu.SemaphoreType.DMA((8 + 2 * rank // ROWS,)),
            pltpu.SemaphoreType.DMA((level.shape[1],)),
        ],
        compiler_params=pltpu.CompilerParams(vmem_limit_bytes=LEAF_IN_KIB * 2**10),
        cost_estimate=cost(4),
        name="leaf_in",
    )(jnp.concatenate([order[:, 0], sizes], axis=0), signal, factor, level_factor)


def unpack_kernel(dense, out_ref):
    width = out_ref.shape[2]

    def body(i, carry):
        rest = dense[2 * width + i]
        half = rest.shape[1] // 2
        out_ref[0, 0, i] = jnp.concatenate([dense[i], rest[:, :half]], axis=1)
        out_ref[0, 1, i] = jnp.concatenate([dense[width + i], rest[:, half:]], axis=1)
        return carry

    lax.fori_loop(0, width, body, 0, unroll=8)


def unpack(dense, shape):
    return pl.pallas_call(
        unpack_kernel,
        out_shape=jax.ShapeDtypeStruct(shape, dense.dtype),
        in_specs=[VMEM],
        out_specs=VMEM,
        compiler_params=pltpu.CompilerParams(vmem_limit_bytes=8 * 2**20),
        cost_estimate=cost(1),
        name="unpack",
    )(dense)


def split_kernel(levels_hbm, *refs):
    count = len(refs) - 1
    copies = [
        pltpu.make_async_copy(levels_hbm.at[1 + k], refs[k], refs[count].at[k])
        for k in range(count)
    ]
    for copy in copies:
        copy.start()
    for copy in copies:
        copy.wait()


def split_levels(level_factor):
    count = level_factor.shape[0] - 1
    level = jax.ShapeDtypeStruct(level_factor.shape[1:], level_factor.dtype)
    return pl.pallas_call(
        split_kernel,
        out_shape=[level] * count,
        in_specs=[HBM],
        out_specs=[VMEM] * count,
        scratch_shapes=[pltpu.SemaphoreType.DMA((count,))],
        compiler_params=pltpu.CompilerParams(vmem_limit_bytes=SPLIT_KIB * 2**10),
        cost_estimate=cost(3),
        name="split_levels",
    )(level_factor)


def flip_kernel(factor, out_ref):
    rows, points = factor.shape
    fill = jnp.zeros((TILE - rows, TILE), factor.dtype)

    def body(chunk, carry):
        base = pl.multiple_of(chunk * TILE, TILE)
        piece = jnp.concatenate([factor[:, pl.ds(base, TILE)], fill], axis=0)
        out_ref[pl.ds(base, TILE), :] = piece.T
        return carry

    lax.fori_loop(0, points // TILE, body, 0, unroll=4)
    tail = LEAFMAX + ROWS
    out_ref[pl.ds(points, tail), :] = jnp.zeros((tail, TILE), factor.dtype)


def flip(factor):
    _, points = factor.shape
    return pl.pallas_call(
        flip_kernel,
        out_shape=jax.ShapeDtypeStruct((points + LEAFMAX + ROWS, TILE), factor.dtype),
        in_specs=[VMEM],
        out_specs=VMEM,
        compiler_params=pltpu.CompilerParams(vmem_limit_bytes=8 * 2**20),
        cost_estimate=cost(4),
        name="flip",
    )(factor)


def mix_pairs(groups, pairs, blocks, weights, put):
    peer_blocks, rank, columns = blocks[0].shape
    half = groups // 2
    half_leaves = half * peer_blocks
    per_part = half_leaves // len(weights)
    me, part_me = lax.axis_index("blk"), lax.axis_index("rhs")
    sign = sign_row(rank, columns).astype(jnp.bfloat16)

    def product(block, stacked):
        h, i = block // half_leaves, block % half_leaves
        source = (i // per_part) ^ part_me
        inner = i % per_part
        own = weights[0][0, h, inner]
        for k in range(1, len(weights)):
            own = jnp.where(source == k, weights[k][0, h, inner], own)
        return jnp.dot(own, stacked, preferred_element_type=jnp.float32).astype(jnp.bfloat16)

    for k, d in enumerate(pairs):

        def body(q, carry):
            first, second = blocks[2 * k][q], blocks[2 * k + 1][q]
            both = jnp.concatenate([first, turned(first, sign)], axis=0)
            also = jnp.concatenate([second, turned(second, sign)], axis=0)
            block = (me ^ d) * peer_blocks + q
            put(2 * k, q, block, product(block, jnp.concatenate([both, also], axis=0)))
            block = (me ^ d ^ half) * peer_blocks + q
            put(2 * k + 1, q, block, product(block, jnp.concatenate([also, both], axis=0)))
            return carry

        lax.fori_loop(0, peer_blocks, body, 0, unroll=min(8, peer_blocks))


def mix_early_kernel(groups, pairs, *refs):
    blocks, weights, out_ref = refs[: 2 * len(pairs)], refs[2 * len(pairs) : -1], refs[-1]

    def put(k, q, block, value):
        out_ref[k, q] = value

    mix_pairs(groups, pairs, blocks, weights, put)


def mix_last_kernel(groups, pairs, early_pairs, target, slots_any, *refs):
    count = len(early_pairs)
    early, blocks = refs[:count], refs[count : count + 2 * len(pairs)]
    weights = refs[count + 2 * len(pairs) : -4]
    out_ref, held, slots_ref, sem = refs[-4:]
    peer_blocks = blocks[0].shape[0]
    me = lax.axis_index("blk")
    copy = pltpu.make_async_copy(slots_any, slots_ref, sem)
    copy.start()

    def put(k, q, block, value):
        held[k, q] = value

    mix_pairs(groups, pairs, blocks, weights, put)
    copy.wait()
    for values, members in zip((*early, held), (*early_pairs, pairs)):
        for k, d in enumerate(e for d in members for e in (d, d ^ (groups // 2))):
            for q in range(peer_blocks):
                out_ref[slots_ref[target, (me ^ d) * peer_blocks + q]] = values[k, q]


def leaf_stage_kernel(groups, pairs, parts, first, last, sizes_any, factor, *refs):
    blocks, weights = refs[: 2 * len(pairs)], refs[2 * len(pairs) : 2 * len(pairs) + parts]
    rest = list(refs[2 * len(pairs) + parts :])
    before = None if first else rest.pop(0)
    out_ref = rest.pop(0)
    held, sizes_ref, starts, sem = rest[:4]
    total = rest[4] if last else out_ref
    peer_blocks, rank, columns = blocks[0].shape
    me = lax.axis_index("blk")
    copy = pltpu.make_async_copy(sizes_any, sizes_ref, sem)
    copy.start()

    def put(k, q, block, value):
        held[k, q] = value

    mix_pairs(groups, pairs, blocks, weights, put)
    if first:
        total[...] = jnp.zeros_like(total)
    else:
        total[...] = before[...]
    copy.wait()
    place_starts(sizes_ref.at[0], starts)
    sign = sign_row(rank, columns).astype(jnp.bfloat16)
    fill = jnp.zeros((TILE - 2 * rank, columns), jnp.bfloat16)
    span = LEAFMAX + ROWS
    row = lax.broadcasted_iota(jnp.int32, (span, columns), 0)
    for k, d in enumerate(e for d in pairs for e in (d, d ^ (groups // 2))):
        for q in range(peer_blocks):
            leaf = (me ^ d) * peer_blocks + q
            start = starts[leaf]
            base = pl.multiple_of(start & ~(ROWS - 1), ROWS)
            low = start - base
            inside = (row >= low) & (row < low + sizes_ref[0, leaf])
            keep = jnp.where(inside, 1.0, 0.0).astype(jnp.bfloat16)
            block = held[k, q]
            stacked = jnp.concatenate([block, turned(block, sign), fill], axis=0)
            sums = jnp.dot(
                factor[pl.ds(base, span), :] * keep, stacked,
                preferred_element_type=jnp.float32,
            )
            total[pl.ds(base, span), :] += sums.astype(jnp.bfloat16)
    if last:
        copy = pltpu.make_async_copy(total.at[pl.ds(0, out_ref.shape[0])], out_ref, sem)
        copy.start()
        copy.wait()


def leaf_stages(sizes, factor, blocks, weights, stages, points):
    groups, parts = len(blocks), len(weights)
    peer_blocks, rank, columns = blocks[0].shape
    span = (factor.shape[0], columns)
    total = None
    for k, pairs in enumerate(stages):
        first, last = k == 0, k == len(stages) - 1
        used = [blocks[d ^ h] for d in pairs for h in (0, groups // 2)]
        before = [] if first else [total]
        total = pl.pallas_call(
            functools.partial(leaf_stage_kernel, groups, pairs, parts, first, last),
            out_shape=jax.ShapeDtypeStruct(
                (points, columns) if last else span, jnp.bfloat16
            ),
            in_specs=[ANY] + [VMEM] * (1 + len(used) + parts + len(before)),
            out_specs=ANY if last else VMEM,
            scratch_shapes=[
                pltpu.VMEM((len(used), peer_blocks, rank, columns), jnp.bfloat16),
                pltpu.SMEM(sizes.shape, jnp.int32),
                pltpu.SMEM((sizes.shape[1],), jnp.int32),
                pltpu.SemaphoreType.DMA,
            ]
            + ([pltpu.VMEM(span, jnp.bfloat16)] if last else []),
            compiler_params=pltpu.CompilerParams(vmem_limit_bytes=16 * 2**20),
            cost_estimate=cost(2),
            name="leaf_stage",
        )(sizes, factor, *used, *weights, *before)
    return total


def mix_level(level, slots, blocks, weights, stages):
    groups, parts = len(blocks), len(weights)
    peer_blocks, rank, columns = blocks[0].shape
    params = pltpu.CompilerParams(vmem_limit_bytes=12 * 2**20)
    used = [[blocks[d ^ h] for d in pairs for h in (0, groups // 2)] for pairs in stages]
    early = []
    for k, pairs in enumerate(stages[:-1]):
        early.append(
            pl.pallas_call(
                functools.partial(mix_early_kernel, groups, pairs),
                out_shape=jax.ShapeDtypeStruct(
                    (2 * len(pairs), peer_blocks, rank, columns), jnp.bfloat16
                ),
                in_specs=[VMEM] * (len(used[k]) + parts),
                out_specs=VMEM,
                compiler_params=params,
                cost_estimate=cost(1),
                name="mix_early",
            )(*used[k], *weights)
        )
    return pl.pallas_call(
        functools.partial(
            mix_last_kernel, groups, stages[-1], stages[:-1], level + 1
        ),
        out_shape=jax.ShapeDtypeStruct((groups * peer_blocks, rank, columns), jnp.bfloat16),
        in_specs=[ANY] + [VMEM] * (len(early) + len(used[-1]) + parts),
        out_specs=VMEM,
        scratch_shapes=[
            pltpu.VMEM((len(used[-1]), peer_blocks, rank, columns), jnp.bfloat16),
            pltpu.SMEM(slots.shape, jnp.int32),
            pltpu.SemaphoreType.DMA,
        ],
        compiler_params=params,
        cost_estimate=cost(1),
        name="mix_last",
    )(slots, *early, *used[-1], *weights)


def stages_of(groups):
    half = groups // 2
    far = [k for k in range(half // 2)]
    near = [half // 2 + k for k in range(half // 2)]
    ordered = [d for pair in zip(near, far) for d in pair]
    first, second = 2 * len(ordered) // 4, 3 * len(ordered) // 4
    return tuple(ordered[:first]), tuple(ordered[first:second]), tuple(ordered[second:])


def issue_order(groups, stages):
    half = groups // 2
    pairs = [d for stage in stages for d in stage]
    middle = [d for d in pairs if d >= half // 2]
    inner = [d for d in pairs if d < half // 2]
    outward = [h for a, b in zip(middle, inner) for h in (b + half, a + half, a)]
    return outward + sorted(d for d in inner if d)


def local(
    groups, parts,
    signal, col_factor, row_factor, level_factor, col_leaf_sizes, row_leaf_sizes, level_order,
):
    levels, leaves = level_order.shape[0], level_order.shape[2]
    peer_blocks = leaves // groups
    stages = stages_of(groups)
    hops = issue_order(groups, stages)

    def shared(own):
        return [
            lax.ppermute(own, "rhs", [(p, p ^ k) for p in range(parts)])
            for k in range(1, parts)
        ]

    outgoing, slots, own, dense = leaf_in(
        col_leaf_sizes, level_order, signal, col_factor, level_factor, groups
    )
    owns = split_levels(level_factor)
    weights = [[own] + [unpack(other, own.shape) for other in shared(dense)]]
    weights += [[own] + shared(own) for own in owns]
    flipped = flip(row_factor)
    for level in range(levels):
        arrived = [outgoing[d * peer_blocks : (d + 1) * peer_blocks] for d in range(groups)]
        for d in hops:
            arrived[d] = lax.ppermute(
                arrived[d], "blk", [(g, g ^ d) for g in range(groups)]
            )
        if level + 1 < levels:
            outgoing = mix_level(level, slots, arrived, weights[level], stages)
    return leaf_stages(row_leaf_sizes, flipped, arrived, weights[-1], stages, signal.shape[0])


def solution(mesh):
    in_specs = (
        P("blk", "rhs"),
        P(None, "blk"),
        P(None, "blk"),
        P(None, "blk", None, "rhs", None, None),
        P("blk", None),
        P("blk", None),
        P(None, "blk", None),
    )
    groups, parts = mesh.shape["blk"], mesh.shape["rhs"]

    def body(*args):
        return local(groups, parts, *args)

    return jax.shard_map(
        body, mesh=mesh, in_specs=in_specs, out_specs=P("blk", "rhs"), check_vma=False
    )
```

profile of v0, /device:TPU:1, one launch (start us, length us, event | category | flops | bytes accessed | tf_op | source)
XLA Modules:
  0.0 194.6 jit_solution(14269900169322263793)
XLA Ops:
  0.7 6.8 %leaf_in.1 = (bf16[128,48,128]{2,1,0:T(8,128)(2,1)S(1)}, s32[4,128]{1,0:T(4,128)S(1)}, bf16[1,2,32,48,192]{4,3,2,1,0:T(8,128)(2,1)S(1)}, bf16[96,48,128]{2,1,0:T(8,128)(2,1)S(1)}) custom-call(s32[5,128]{1,0:T(8,128)S(1)} %pad_add_fusion.leaves_ref, bf16[8192,128]{1,0:T(8,128)(2,1)} %signal_hbm.1, bf16[96,8192]{1,0:T(8,128)(2,1)} %factor_hbm.1, ...), custom_call_target="tpu_custom_call" | custom-call | flops 40000000 | tf_op jit(solution)/shard_map/leaf_in/pallas_call | solution.py:132
  16.1 4.0 %collective-permute-start.3 = (bf16[8,48,128]{2,1,0:T(8,128)(2,1)S(1)}, bf16[8,48,128]{2,1,0:T(8,128)(2,1)S(1)}, u32[]{:S(2)}, u32[]{:S(2)}) collective-permute-start(bf16[8,48,128]{2,1,0:T(8,128)(2,1)S(1)} %get-tuple-element.78), channel_id=1, source_target_pairs={{0,10},{2,8},{4,14},{6,12},{8,2},{10,0},{12,6},{14,4},{16,26},{18,... | collective-permute-start | bytes 294920 | tf_op jit(solution)/shard_map/ppermute | solution.py:455
  20.1 4.5 %collective-permute-start.4 = (bf16[8,48,128]{2,1,0:T(8,128)(2,1)S(1)}, bf16[8,48,128]{2,1,0:T(8,128)(2,1)S(1)}, u32[]{:S(2)}, u32[]{:S(2)}) collective-permute-start(bf16[8,48,128]{2,1,0:T(8,128)(2,1)S(1)} %get-tuple-element.77), channel_id=1, source_target_pairs={{0,26},{2,24},{4,30},{6,28},{8,18},{10,16},{12,22},{14,20},{16,10}... | collective-permute-start | bytes 294920 | tf_op jit(solution)/shard_map/ppermute | solution.py:455
  28.2 6.7 %collective-permute-start.11 = (bf16[8,48,128]{2,1,0:T(8,128)(2,1)S(1)}, bf16[8,48,128]{2,1,0:T(8,128)(2,1)S(1)}, u32[]{:S(2)}, u32[]{:S(2)}) collective-permute-start(bf16[8,48,128]{2,1,0:T(8,128)(2,1)S(1)} %get-tuple-element.71), channel_id=1, source_target_pairs={{0,20},{2,22},{4,16},{6,18},{8,28},{10,30},{12,24},{14,26},{16,4},... | collective-permute-start | bytes 294920 | tf_op jit(solution)/shard_map/ppermute | solution.py:455
  35.2 2.5 %collective-permute-start.9 = (bf16[8,48,128]{2,1,0:T(8,128)(2,1)S(1)}, bf16[8,48,128]{2,1,0:T(8,128)(2,1)S(1)}, u32[]{:S(2)}, u32[]{:S(2)}) collective-permute-start(bf16[8,48,128]{2,1,0:T(8,128)(2,1)S(1)} %get-tuple-element.73), channel_id=1, source_target_pairs={{0,28},{2,30},{4,24},{6,26},{8,20},{10,22},{12,16},{14,18},{16,12}... | collective-permute-start | bytes 294920 | tf_op jit(solution)/shard_map/ppermute | solution.py:455
  40.6 3.1 %collective-permute-start.13 = (bf16[8,48,128]{2,1,0:T(8,128)(2,1)S(1)}, bf16[8,48,128]{2,1,0:T(8,128)(2,1)S(1)}, u32[]{:S(2)}, u32[]{:S(2)}) collective-permute-start(bf16[8,48,128]{2,1,0:T(8,128)(2,1)S(1)} %get-tuple-element.69), channel_id=1, source_target_pairs={{0,30},{2,28},{4,26},{6,24},{8,22},{10,20},{12,18},{14,16},{16,14}... | collective-permute-start | bytes 294920 | tf_op jit(solution)/shard_map/ppermute | solution.py:455
  43.7 3.9 %collective-permute-start.14 = (bf16[8,48,128]{2,1,0:T(8,128)(2,1)S(1)}, bf16[8,48,128]{2,1,0:T(8,128)(2,1)S(1)}, u32[]{:S(2)}, u32[]{:S(2)}) collective-permute-start(bf16[8,48,128]{2,1,0:T(8,128)(2,1)S(1)} %get-tuple-element.68), channel_id=1, source_target_pairs={{0,6},{2,4},{4,2},{6,0},{8,14},{10,12},{12,10},{14,8},{16,22},{18,... | collective-permute-start | bytes 294920 | tf_op jit(solution)/shard_map/ppermute | solution.py:455
  47.6 5.5 %collective-permute-start.15 = (bf16[8,48,128]{2,1,0:T(8,128)(2,1)S(1)}, bf16[8,48,128]{2,1,0:T(8,128)(2,1)S(1)}, u32[]{:S(2)}, u32[]{:S(2)}) collective-permute-start(bf16[8,48,128]{2,1,0:T(8,128)(2,1)S(1)} %get-tuple-element.67), channel_id=1, source_target_pairs={{0,22},{2,20},{4,18},{6,16},{8,30},{10,28},{12,26},{14,24},{16,6},... | collective-permute-start | bytes 294920 | tf_op jit(solution)/shard_map/ppermute | solution.py:455
  59.1 3.9 %collective-permute-start.25 = (bf16[8,48,128]{2,1,0:T(8,128)(2,1)S(1)}, bf16[8,48,128]{2,1,0:T(8,128)(2,1)S(1)}, u32[]{:S(2)}, u32[]{:S(2)}) collective-permute-start(bf16[8,48,128]{2,1,0:T(8,128)(2,1)S(1)} %get-tuple-element.57), channel_id=1, source_target_pairs={{0,28},{2,30},{4,24},{6,26},{8,20},{10,22},{12,16},{14,18},{16,12}... | collective-permute-start | bytes 294920 | tf_op jit(solution)/shard_map/ppermute | solution.py:455
  63.0 6.0 %collective-permute-done.23.refs_9_.refs_5_.refs_7_ = bf16[1,2,32,48,192]{4,3,2,1,0:T(8,128)(2,1)S(1)} collective-permute-done((bf16[1,2,32,48,192]{4,3,2,1,0:T(8,128)(2,1)S(1)}, bf16[1,2,32,48,192]{4,3,2,1,0:T(8,128)(2,1)S(1)}, u32[]{:S(2)}, u32[]{:S(2)}) %collective-permute-start.23) | collective-permute-done | bytes 1179680 | tf_op jit(solution)/shard_map/ppermute | solution.py:441
  69.0 3.2 %collective-permute-start.27 = (bf16[8,48,128]{2,1,0:T(8,128)(2,1)S(1)}, bf16[8,48,128]{2,1,0:T(8,128)(2,1)S(1)}, u32[]{:S(2)}, u32[]{:S(2)}) collective-permute-start(bf16[8,48,128]{2,1,0:T(8,128)(2,1)S(1)} %get-tuple-element.55), channel_id=1, source_target_pairs={{0,20},{2,22},{4,16},{6,18},{8,28},{10,30},{12,24},{14,26},{16,4},... | collective-permute-start | bytes 294920 | tf_op jit(solution)/shard_map/ppermute | solution.py:455
  74.9 9.1 %collective-permute-start.19 = (bf16[8,48,128]{2,1,0:T(8,128)(2,1)S(1)}, bf16[8,48,128]{2,1,0:T(8,128)(2,1)S(1)}, u32[]{:S(2)}, u32[]{:S(2)}) collective-permute-start(bf16[8,48,128]{2,1,0:T(8,128)(2,1)S(1)} %get-tuple-element.62), channel_id=1, source_target_pairs={{0,10},{2,8},{4,14},{6,12},{8,2},{10,0},{12,6},{14,4},{16,26},{18,... | collective-permute-start | bytes 294920 | tf_op jit(solution)/shard_map/ppermute | solution.py:455
  84.0 2.8 %collective-permute-start.20 = (bf16[8,48,128]{2,1,0:T(8,128)(2,1)S(1)}, bf16[8,48,128]{2,1,0:T(8,128)(2,1)S(1)}, u32[]{:S(2)}, u32[]{:S(2)}) collective-permute-start(bf16[8,48,128]{2,1,0:T(8,128)(2,1)S(1)} %get-tuple-element.61), channel_id=1, source_target_pairs={{0,26},{2,24},{4,30},{6,28},{8,18},{10,16},{12,22},{14,20},{16,10}... | collective-permute-start | bytes 294920 | tf_op jit(solution)/shard_map/ppermute | solution.py:455
  92.4 2.7 %collective-permute-start.29 = (bf16[8,48,128]{2,1,0:T(8,128)(2,1)S(1)}, bf16[8,48,128]{2,1,0:T(8,128)(2,1)S(1)}, u32[]{:S(2)}, u32[]{:S(2)}) collective-permute-start(bf16[8,48,128]{2,1,0:T(8,128)(2,1)S(1)} %get-tuple-element.53), channel_id=1, source_target_pairs={{0,30},{2,28},{4,26},{6,24},{8,22},{10,20},{12,18},{14,16},{16,14}... | collective-permute-start | bytes 294920 | tf_op jit(solution)/shard_map/ppermute | solution.py:455
  95.1 3.1 %collective-permute-start.30 = (bf16[8,48,128]{2,1,0:T(8,128)(2,1)S(1)}, bf16[8,48,128]{2,1,0:T(8,128)(2,1)S(1)}, u32[]{:S(2)}, u32[]{:S(2)}) collective-permute-start(bf16[8,48,128]{2,1,0:T(8,128)(2,1)S(1)} %get-tuple-element.52), channel_id=1, source_target_pairs={{0,6},{2,4},{4,2},{6,0},{8,14},{10,12},{12,10},{14,8},{16,22},{18,... | collective-permute-start | bytes 294920 | tf_op jit(solution)/shard_map/ppermute | solution.py:455
  98.2 2.4 %collective-permute-done.28.refs_2_ = bf16[8,48,128]{2,1,0:T(8,128)(2,1)S(1)} collective-permute-done((bf16[8,48,128]{2,1,0:T(8,128)(2,1)S(1)}, bf16[8,48,128]{2,1,0:T(8,128)(2,1)S(1)}, u32[]{:S(2)}, u32[]{:S(2)}) %collective-permute-start.28) | collective-permute-done | bytes 98336 | tf_op jit(solution)/shard_map/ppermute | solution.py:455
  103.9 3.2 %collective-permute-done.31.refs_5_ = bf16[8,48,128]{2,1,0:T(8,128)(2,1)S(1)} collective-permute-done((bf16[8,48,128]{2,1,0:T(8,128)(2,1)S(1)}, bf16[8,48,128]{2,1,0:T(8,128)(2,1)S(1)}, u32[]{:S(2)}, u32[]{:S(2)}) %collective-permute-start.31) | collective-permute-done | bytes 98336 | tf_op jit(solution)/shard_map/ppermute | solution.py:455
  108.9 2.6 %collective-permute-start.41 = (bf16[8,48,128]{2,1,0:T(8,128)(2,1)S(1)}, bf16[8,48,128]{2,1,0:T(8,128)(2,1)S(1)}, u32[]{:S(2)}, u32[]{:S(2)}) collective-permute-start(bf16[8,48,128]{2,1,0:T(8,128)(2,1)S(1)} %get-tuple-element.41), channel_id=1, source_target_pairs={{0,28},{2,30},{4,24},{6,26},{8,20},{10,22},{12,16},{14,18},{16,12}... | collective-permute-start | bytes 294920 | tf_op jit(solution)/shard_map/ppermute | solution.py:455
  113.8 2.7 %collective-permute-done.41.refs_1_ = bf16[8,48,128]{2,1,0:T(8,128)(2,1)S(1)} collective-permute-done((bf16[8,48,128]{2,1,0:T(8,128)(2,1)S(1)}, bf16[8,48,128]{2,1,0:T(8,128)(2,1)S(1)}, u32[]{:S(2)}, u32[]{:S(2)}) %collective-permute-start.41) | collective-permute-done | bytes 98336 | tf_op jit(solution)/shard_map/ppermute | solution.py:455
  118.0 3.3 %collective-permute-start.34 = (bf16[8,48,128]{2,1,0:T(8,128)(2,1)S(1)}, bf16[8,48,128]{2,1,0:T(8,128)(2,1)S(1)}, u32[]{:S(2)}, u32[]{:S(2)}) collective-permute-start(bf16[8,48,128]{2,1,0:T(8,128)(2,1)S(1)} %get-tuple-element.47), channel_id=1, source_target_pairs={{0,16},{2,18},{4,20},{6,22},{8,24},{10,26},{12,28},{14,30},{16,0},... | collective-permute-start | bytes 294920 | tf_op jit(solution)/shard_map/ppermute | solution.py:455
  122.3 4.3 %collective-permute-start.36 = (bf16[8,48,128]{2,1,0:T(8,128)(2,1)S(1)}, bf16[8,48,128]{2,1,0:T(8,128)(2,1)S(1)}, u32[]{:S(2)}, u32[]{:S(2)}) collective-permute-start(bf16[8,48,128]{2,1,0:T(8,128)(2,1)S(1)} %get-tuple-element.45), channel_id=1, source_target_pairs={{0,26},{2,24},{4,30},{6,28},{8,18},{10,16},{12,22},{14,20},{16,10}... | collective-permute-start | bytes 294920 | tf_op jit(solution)/shard_map/ppermute | solution.py:455
  126.7 5.9 %collective-permute-done.34.refs_3_ = bf16[8,48,128]{2,1,0:T(8,128)(2,1)S(1)} collective-permute-done((bf16[8,48,128]{2,1,0:T(8,128)(2,1)S(1)}, bf16[8,48,128]{2,1,0:T(8,128)(2,1)S(1)}, u32[]{:S(2)}, u32[]{:S(2)}) %collective-permute-start.34) | collective-permute-done | bytes 98336 | tf_op jit(solution)/shard_map/ppermute | solution.py:455
  132.5 2.6 %collective-permute-start.44 = (bf16[8,48,128]{2,1,0:T(8,128)(2,1)S(1)}, bf16[8,48,128]{2,1,0:T(8,128)(2,1)S(1)}, u32[]{:S(2)}, u32[]{:S(2)}) collective-permute-start(bf16[8,48,128]{2,1,0:T(8,128)(2,1)S(1)} %get-tuple-element.38), channel_id=1, source_target_pairs={{0,14},{2,12},{4,10},{6,8},{8,6},{10,4},{12,2},{14,0},{16,30},{18,... | collective-permute-start | bytes 294920 | tf_op jit(solution)/shard_map/ppermute | solution.py:455
  135.2 2.4 %collective-permute-start.45 = (bf16[8,48,128]{2,1,0:T(8,128)(2,1)S(1)}, bf16[8,48,128]{2,1,0:T(8,128)(2,1)S(1)}, u32[]{:S(2)}, u32[]{:S(2)}) collective-permute-start(bf16[8,48,128]{2,1,0:T(8,128)(2,1)S(1)} %get-tuple-element.37), channel_id=1, source_target_pairs={{0,30},{2,28},{4,26},{6,24},{8,22},{10,20},{12,18},{14,16},{16,14}... | collective-permute-start | bytes 294920 | tf_op jit(solution)/shard_map/ppermute | solution.py:455
  144.2 3.5 %collective-permute-done.47.refs_5_ = bf16[8,48,128]{2,1,0:T(8,128)(2,1)S(1)} collective-permute-done((bf16[8,48,128]{2,1,0:T(8,128)(2,1)S(1)}, bf16[8,48,128]{2,1,0:T(8,128)(2,1)S(1)}, u32[]{:S(2)}, u32[]{:S(2)}) %collective-permute-start.47) | collective-permute-done | bytes 98336 | tf_op jit(solution)/shard_map/ppermute | solution.py:455
  156.3 6.4 %collective-permute-start.63 = (bf16[8,48,128]{2,1,0:T(8,128)(2,1)S(1)}, bf16[8,48,128]{2,1,0:T(8,128)(2,1)S(1)}, u32[]{:S(2)}, u32[]{:S(2)}) collective-permute-start(bf16[8,48,128]{2,1,0:T(8,128)(2,1)S(1)} %get-tuple-element.19), channel_id=1, source_target_pairs={{0,18},{2,16},{4,22},{6,20},{8,26},{10,24},{12,30},{14,28},{16,2},... | collective-permute-start | bytes 294920 | tf_op jit(solution)/shard_map/ppermute | solution.py:455
  164.7 2.5 %collective-permute-start.55 = (bf16[8,48,128]{2,1,0:T(8,128)(2,1)S(1)}, bf16[8,48,128]{2,1,0:T(8,128)(2,1)S(1)}, u32[]{:S(2)}, u32[]{:S(2)}) collective-permute-start(bf16[8,48,128]{2,1,0:T(8,128)(2,1)S(1)} %get-tuple-element.28), channel_id=1, source_target_pairs={{0,4},{2,6},{4,0},{6,2},{8,12},{10,14},{12,8},{14,10},{16,20},{18,... | collective-permute-start | bytes 294920 | tf_op jit(solution)/shard_map/ppermute | solution.py:455
  167.2 5.1 %collective-permute-start.56 = (bf16[8,48,128]{2,1,0:T(8,128)(2,1)S(1)}, bf16[8,48,128]{2,1,0:T(8,128)(2,1)S(1)}, u32[]{:S(2)}, u32[]{:S(2)}) collective-permute-start(bf16[8,48,128]{2,1,0:T(8,128)(2,1)S(1)} %get-tuple-element.27), channel_id=1, source_target_pairs={{0,20},{2,22},{4,16},{6,18},{8,28},{10,30},{12,24},{14,26},{16,4},... | collective-permute-start | bytes 294920 | tf_op jit(solution)/shard_map/ppermute | solution.py:455
  177.0 5.6 %collective-permute-start.51 = (bf16[8,48,128]{2,1,0:T(8,128)(2,1)S(1)}, bf16[8,48,128]{2,1,0:T(8,128)(2,1)S(1)}, u32[]{:S(2)}, u32[]{:S(2)}) collective-permute-start(bf16[8,48,128]{2,1,0:T(8,128)(2,1)S(1)} %get-tuple-element.31), channel_id=1, source_target_pairs={{0,22},{2,20},{4,18},{6,16},{8,30},{10,28},{12,26},{14,24},{16,6},... | collective-permute-start | bytes 294920 | tf_op jit(solution)/shard_map/ppermute | solution.py:455
  184.4 3.8 %leaf_stage.3.refs_6_ = bf16[8336,128]{1,0:T(8,128)(2,1)S(1)} custom-call(s32[1,128]{1,0:T(1,128)S(1)} %copy-done.1, bf16[8336,128]{1,0:T(8,128)(2,1)S(1)} %flip.1.factor, bf16[8,48,128]{2,1,0:T(8,128)(2,1)S(1)} %collective-permute-done.57.refs_0_, bf16[8,48,128]{2,1,0:T(8,128)(2,1)S(1)} %collective-permute-done.58.refs_1_, ...), custom_call_target="tpu_custom_call" | custom-call | flops 20000000 | tf_op jit(solution)/shard_map/leaf_stage/pallas_call | solution.py:353
  188.2 2.4 %leaf_stage.4.refs_6_ = bf16[8336,128]{1,0:T(8,128)(2,1)S(1)} custom-call(s32[1,128]{1,0:T(1,128)S(1)} %copy-done.1, bf16[8336,128]{1,0:T(8,128)(2,1)S(1)} %flip.1.factor, bf16[8,48,128]{2,1,0:T(8,128)(2,1)S(1)} %collective-permute-done.53.refs_0_, bf16[8,48,128]{2,1,0:T(8,128)(2,1)S(1)} %collective-permute-done.54.refs_1_, ...), custom_call_target="tpu_custom_call" | custom-call | flops 20000000 | tf_op jit(solution)/shard_map/leaf_stage/pallas_call | solution.py:353
  190.7 3.8 %leaf_stage.5 = bf16[8192,128]{1,0:T(8,128)(2,1)} custom-call(s32[1,128]{1,0:T(1,128)S(1)} %copy-done.1, bf16[8336,128]{1,0:T(8,128)(2,1)S(1)} %flip.1.factor, bf16[8,48,128]{2,1,0:T(8,128)(2,1)S(1)} %collective-permute-done.48.refs_0_, bf16[8,48,128]{2,1,0:T(8,128)(2,1)S(1)} %collective-permute-done.49.refs_1_, ...), custom_call_target="tpu_custom_call" | custom-call | flops 20000000 | tf_op jit(solution)/shard_map/leaf_stage/pallas_call | solution.py:353
  (121 shorter events, 63.5 us)
Async XLA Ops:
  7.5 45.6 %collective-permute-start.7 = (bf16[96,48,128]{2,1,0:T(8,128)(2,1)S(1)}, bf16[96,48,128]{2,1,0:T(8,128)(2,1)S(1)}, u32[]{:S(2)}, u32[]{:S(2)}) collective-permute-start(bf16[96,48,128]{2,1,0:T(8,128)(2,1)S(1)} %get-tuple-element.15), channel_id=1, source_target_pairs={{0,1},{1,0},{2,3},{3,2},{4,5},{5,4},{6,7},{7,6},{8,9},{9,8},{10,11... | collective-permute-start | bytes 3538952 | tf_op jit(solution)/shard_map/ppermute | solution.py:441
  12.0 57.0 %collective-permute-start.23 = (bf16[1,2,32,48,192]{4,3,2,1,0:T(8,128)(2,1)S(1)}, bf16[1,2,32,48,192]{4,3,2,1,0:T(8,128)(2,1)S(1)}, u32[]{:S(2)}, u32[]{:S(2)}) collective-permute-start(bf16[1,2,32,48,192]{4,3,2,1,0:T(8,128)(2,1)S(1)} %get-tuple-element.16.refs_8_.refs_4_.refs_6_), channel_id=1, source_target_pairs={{0,1},{1,0},{2,3},{3,2},{4,5},{5,4},{6,7},{7,6},{8,9},{9,8},{10,11... | collective-permute-start | bytes 3538952 | tf_op jit(solution)/shard_map/ppermute | solution.py:441
  28.2 11.1 %collective-permute-start.11 = (bf16[8,48,128]{2,1,0:T(8,128)(2,1)S(1)}, bf16[8,48,128]{2,1,0:T(8,128)(2,1)S(1)}, u32[]{:S(2)}, u32[]{:S(2)}) collective-permute-start(bf16[8,48,128]{2,1,0:T(8,128)(2,1)S(1)} %get-tuple-element.71), channel_id=1, source_target_pairs={{0,20},{2,22},{4,16},{6,18},{8,28},{10,30},{12,24},{14,26},{16,4},... | collective-permute-start | bytes 294920 | tf_op jit(solution)/shard_map/ppermute | solution.py:455
  40.6 16.6 %collective-permute-start.13 = (bf16[8,48,128]{2,1,0:T(8,128)(2,1)S(1)}, bf16[8,48,128]{2,1,0:T(8,128)(2,1)S(1)}, u32[]{:S(2)}, u32[]{:S(2)}) collective-permute-start(bf16[8,48,128]{2,1,0:T(8,128)(2,1)S(1)} %get-tuple-element.69), channel_id=1, source_target_pairs={{0,30},{2,28},{4,26},{6,24},{8,22},{10,20},{12,18},{14,16},{16,14}... | collective-permute-start | bytes 294920 | tf_op jit(solution)/shard_map/ppermute | solution.py:455
  43.7 13.5 %collective-permute-start.14 = (bf16[8,48,128]{2,1,0:T(8,128)(2,1)S(1)}, bf16[8,48,128]{2,1,0:T(8,128)(2,1)S(1)}, u32[]{:S(2)}, u32[]{:S(2)}) collective-permute-start(bf16[8,48,128]{2,1,0:T(8,128)(2,1)S(1)} %get-tuple-element.68), channel_id=1, source_target_pairs={{0,6},{2,4},{4,2},{6,0},{8,14},{10,12},{12,10},{14,8},{16,22},{18,... | collective-permute-start | bytes 294920 | tf_op jit(solution)/shard_map/ppermute | solution.py:455
  53.1 58.4 %collective-permute-start.39 = (bf16[1,2,32,48,192]{4,3,2,1,0:T(8,128)(2,1)S(1)}, bf16[1,2,32,48,192]{4,3,2,1,0:T(8,128)(2,1)S(1)}, u32[]{:S(2)}, u32[]{:S(2)}) collective-permute-start(bf16[1,2,32,48,192]{4,3,2,1,0:T(8,128)(2,1)S(1)} %get-tuple-element.17.refs_8_.refs_4_.refs_6_), channel_id=1, source_target_pairs={{0,1},{1,0},{2,3},{3,2},{4,5},{5,4},{6,7},{7,6},{8,9},{9,8},{10,11... | collective-permute-start | bytes 3538952 | tf_op jit(solution)/shard_map/ppermute | solution.py:441
  58.8 13.4 %collective-permute-start.24 = (bf16[8,48,128]{2,1,0:T(8,128)(2,1)S(1)}, bf16[8,48,128]{2,1,0:T(8,128)(2,1)S(1)}, u32[]{:S(2)}, u32[]{:S(2)}) collective-permute-start(bf16[8,48,128]{2,1,0:T(8,128)(2,1)S(1)} %get-tuple-element.58), channel_id=1, source_target_pairs={{0,12},{2,14},{4,8},{6,10},{8,4},{10,6},{12,0},{14,2},{16,28},{18,... | collective-permute-start | bytes 294920 | tf_op jit(solution)/shard_map/ppermute | solution.py:455
  59.1 14.5 %collective-permute-start.25 = (bf16[8,48,128]{2,1,0:T(8,128)(2,1)S(1)}, bf16[8,48,128]{2,1,0:T(8,128)(2,1)S(1)}, u32[]{:S(2)}, u32[]{:S(2)}) collective-permute-start(bf16[8,48,128]{2,1,0:T(8,128)(2,1)S(1)} %get-tuple-element.57), channel_id=1, source_target_pairs={{0,28},{2,30},{4,24},{6,26},{8,20},{10,22},{12,16},{14,18},{16,12}... | collective-permute-start | bytes 294920 | tf_op jit(solution)/shard_map/ppermute | solution.py:455
  63.0 10.5 %collective-permute-start.26 = (bf16[8,48,128]{2,1,0:T(8,128)(2,1)S(1)}, bf16[8,48,128]{2,1,0:T(8,128)(2,1)S(1)}, u32[]{:S(2)}, u32[]{:S(2)}) collective-permute-start(bf16[8,48,128]{2,1,0:T(8,128)(2,1)S(1)} %get-tuple-element.56), channel_id=1, source_target_pairs={{0,4},{2,6},{4,0},{6,2},{8,12},{10,14},{12,8},{14,10},{16,20},{18,... | collective-permute-start | bytes 294920 | tf_op jit(solution)/shard_map/ppermute | solution.py:455
  72.2 11.8 %collective-permute-start.16 = (bf16[8,48,128]{2,1,0:T(8,128)(2,1)S(1)}, bf16[8,48,128]{2,1,0:T(8,128)(2,1)S(1)}, u32[]{:S(2)}, u32[]{:S(2)}) collective-permute-start(bf16[8,48,128]{2,1,0:T(8,128)(2,1)S(1)} %get-tuple-element.66), channel_id=1, source_target_pairs={{0,8},{2,10},{4,12},{6,14},{8,0},{10,2},{12,4},{14,6},{16,24},{18,... | collective-permute-start | bytes 294920 | tf_op jit(solution)/shard_map/ppermute | solution.py:455
  73.5 13.3 %collective-permute-start.17 = (bf16[8,48,128]{2,1,0:T(8,128)(2,1)S(1)}, bf16[8,48,128]{2,1,0:T(8,128)(2,1)S(1)}, u32[]{:S(2)}, u32[]{:S(2)}) collective-permute-start(bf16[8,48,128]{2,1,0:T(8,128)(2,1)S(1)} %get-tuple-element.65), channel_id=1, source_target_pairs={{0,24},{2,26},{4,28},{6,30},{8,16},{10,18},{12,20},{14,22},{16,8},... | collective-permute-start | bytes 294920 | tf_op jit(solution)/shard_map/ppermute | solution.py:455
  73.5 14.5 %collective-permute-start.18 = (bf16[8,48,128]{2,1,0:T(8,128)(2,1)S(1)}, bf16[8,48,128]{2,1,0:T(8,128)(2,1)S(1)}, u32[]{:S(2)}, u32[]{:S(2)}) collective-permute-start(bf16[8,48,128]{2,1,0:T(8,128)(2,1)S(1)} %get-tuple-element.63), channel_id=1, source_target_pairs={{0,16},{2,18},{4,20},{6,22},{8,24},{10,26},{12,28},{14,30},{16,0},... | collective-permute-start | bytes 294920 | tf_op jit(solution)/shard_map/ppermute | solution.py:455
  74.9 13.8 %collective-permute-start.19 = (bf16[8,48,128]{2,1,0:T(8,128)(2,1)S(1)}, bf16[8,48,128]{2,1,0:T(8,128)(2,1)S(1)}, u32[]{:S(2)}, u32[]{:S(2)}) collective-permute-start(bf16[8,48,128]{2,1,0:T(8,128)(2,1)S(1)} %get-tuple-element.62), channel_id=1, source_target_pairs={{0,10},{2,8},{4,14},{6,12},{8,2},{10,0},{12,6},{14,4},{16,26},{18,... | collective-permute-start | bytes 294920 | tf_op jit(solution)/shard_map/ppermute | solution.py:455
  86.8 66.9 %collective-permute-start.52 = (bf16[1,2,32,48,192]{4,3,2,1,0:T(8,128)(2,1)S(1)}, bf16[1,2,32,48,192]{4,3,2,1,0:T(8,128)(2,1)S(1)}, u32[]{:S(2)}, u32[]{:S(2)}) collective-permute-start(bf16[1,2,32,48,192]{4,3,2,1,0:T(8,128)(2,1)S(1)} %get-tuple-element.18.refs_8_.refs_4_), channel_id=1, source_target_pairs={{0,1},{1,0},{2,3},{3,2},{4,5},{5,4},{6,7},{7,6},{8,9},{9,8},{10,11... | collective-permute-start | bytes 3538952 | tf_op jit(solution)/shard_map/ppermute | solution.py:441
  111.5 10.8 %collective-permute-start.43 = (bf16[8,48,128]{2,1,0:T(8,128)(2,1)S(1)}, bf16[8,48,128]{2,1,0:T(8,128)(2,1)S(1)}, u32[]{:S(2)}, u32[]{:S(2)}) collective-permute-start(bf16[8,48,128]{2,1,0:T(8,128)(2,1)S(1)} %get-tuple-element.39), channel_id=1, source_target_pairs={{0,20},{2,22},{4,16},{6,18},{8,28},{10,30},{12,24},{14,26},{16,4},... | collective-permute-start | bytes 294920 | tf_op jit(solution)/shard_map/ppermute | solution.py:455
  118.0 14.5 %collective-permute-start.34 = (bf16[8,48,128]{2,1,0:T(8,128)(2,1)S(1)}, bf16[8,48,128]{2,1,0:T(8,128)(2,1)S(1)}, u32[]{:S(2)}, u32[]{:S(2)}) collective-permute-start(bf16[8,48,128]{2,1,0:T(8,128)(2,1)S(1)} %get-tuple-element.47), channel_id=1, source_target_pairs={{0,16},{2,18},{4,20},{6,22},{8,24},{10,26},{12,28},{14,30},{16,0},... | collective-permute-start | bytes 294920 | tf_op jit(solution)/shard_map/ppermute | solution.py:455
  122.3 10.2 %collective-permute-start.35 = (bf16[8,48,128]{2,1,0:T(8,128)(2,1)S(1)}, bf16[8,48,128]{2,1,0:T(8,128)(2,1)S(1)}, u32[]{:S(2)}, u32[]{:S(2)}) collective-permute-start(bf16[8,48,128]{2,1,0:T(8,128)(2,1)S(1)} %get-tuple-element.46), channel_id=1, source_target_pairs={{0,10},{2,8},{4,14},{6,12},{8,2},{10,0},{12,6},{14,4},{16,26},{18,... | collective-permute-start | bytes 294920 | tf_op jit(solution)/shard_map/ppermute | solution.py:455
  122.3 12.9 %collective-permute-start.36 = (bf16[8,48,128]{2,1,0:T(8,128)(2,1)S(1)}, bf16[8,48,128]{2,1,0:T(8,128)(2,1)S(1)}, u32[]{:S(2)}, u32[]{:S(2)}) collective-permute-start(bf16[8,48,128]{2,1,0:T(8,128)(2,1)S(1)} %get-tuple-element.45), channel_id=1, source_target_pairs={{0,26},{2,24},{4,30},{6,28},{8,18},{10,16},{12,22},{14,20},{16,10}... | collective-permute-start | bytes 294920 | tf_op jit(solution)/shard_map/ppermute | solution.py:455
  126.7 10.9 %collective-permute-start.37 = (bf16[8,48,128]{2,1,0:T(8,128)(2,1)S(1)}, bf16[8,48,128]{2,1,0:T(8,128)(2,1)S(1)}, u32[]{:S(2)}, u32[]{:S(2)}) collective-permute-start(bf16[8,48,128]{2,1,0:T(8,128)(2,1)S(1)} %get-tuple-element.44), channel_id=1, source_target_pairs={{0,2},{2,0},{4,6},{6,4},{8,10},{10,8},{12,14},{14,12},{16,18},{18,... | collective-permute-start | bytes 294920 | tf_op jit(solution)/shard_map/ppermute | solution.py:455
  151.4 11.2 %collective-permute-start.59 = (bf16[8,48,128]{2,1,0:T(8,128)(2,1)S(1)}, bf16[8,48,128]{2,1,0:T(8,128)(2,1)S(1)}, u32[]{:S(2)}, u32[]{:S(2)}) collective-permute-start(bf16[8,48,128]{2,1,0:T(8,128)(2,1)S(1)} %get-tuple-element.23), channel_id=1, source_target_pairs={{0,16},{2,18},{4,20},{6,22},{8,24},{10,26},{12,28},{14,30},{16,0},... | collective-permute-start | bytes 294920 | tf_op jit(solution)/shard_map/ppermute | solution.py:455
  152.1 10.5 %collective-permute-start.60 = (bf16[8,48,128]{2,1,0:T(8,128)(2,1)S(1)}, bf16[8,48,128]{2,1,0:T(8,128)(2,1)S(1)}, u32[]{:S(2)}, u32[]{:S(2)}) collective-permute-start(bf16[8,48,128]{2,1,0:T(8,128)(2,1)S(1)} %get-tuple-element.22), channel_id=1, source_target_pairs={{0,10},{2,8},{4,14},{6,12},{8,2},{10,0},{12,6},{14,4},{16,26},{18,... | collective-permute-start | bytes 294920 | tf_op jit(solution)/shard_map/ppermute | solution.py:455
  153.8 10.9 %collective-permute-start.61 = (bf16[8,48,128]{2,1,0:T(8,128)(2,1)S(1)}, bf16[8,48,128]{2,1,0:T(8,128)(2,1)S(1)}, u32[]{:S(2)}, u32[]{:S(2)}) collective-permute-start(bf16[8,48,128]{2,1,0:T(8,128)(2,1)S(1)} %get-tuple-element.21), channel_id=1, source_target_pairs={{0,26},{2,24},{4,30},{6,28},{8,18},{10,16},{12,22},{14,20},{16,10}... | collective-permute-start | bytes 294920 | tf_op jit(solution)/shard_map/ppermute | solution.py:455
  155.3 11.9 %collective-permute-start.62 = (bf16[8,48,128]{2,1,0:T(8,128)(2,1)S(1)}, bf16[8,48,128]{2,1,0:T(8,128)(2,1)S(1)}, u32[]{:S(2)}, u32[]{:S(2)}) collective-permute-start(bf16[8,48,128]{2,1,0:T(8,128)(2,1)S(1)} %get-tuple-element.20), channel_id=1, source_target_pairs={{0,2},{2,0},{4,6},{6,4},{8,10},{10,8},{12,14},{14,12},{16,18},{18,... | collective-permute-start | bytes 294920 | tf_op jit(solution)/shard_map/ppermute | solution.py:455
  156.3 16.0 %collective-permute-start.63 = (bf16[8,48,128]{2,1,0:T(8,128)(2,1)S(1)}, bf16[8,48,128]{2,1,0:T(8,128)(2,1)S(1)}, u32[]{:S(2)}, u32[]{:S(2)}) collective-permute-start(bf16[8,48,128]{2,1,0:T(8,128)(2,1)S(1)} %get-tuple-element.19), channel_id=1, source_target_pairs={{0,18},{2,16},{4,22},{6,20},{8,26},{10,24},{12,30},{14,28},{16,2},... | collective-permute-start | bytes 294920 | tf_op jit(solution)/shard_map/ppermute | solution.py:455
  162.6 11.0 %collective-permute-start.53 = (bf16[8,48,128]{2,1,0:T(8,128)(2,1)S(1)}, bf16[8,48,128]{2,1,0:T(8,128)(2,1)S(1)}, u32[]{:S(2)}, u32[]{:S(2)}) collective-permute-start(bf16[8,48,128]{2,1,0:T(8,128)(2,1)S(1)} %get-tuple-element.30), channel_id=1, source_target_pairs={{0,12},{2,14},{4,8},{6,10},{8,4},{10,6},{12,0},{14,2},{16,28},{18,... | collective-permute-start | bytes 294920 | tf_op jit(solution)/shard_map/ppermute | solution.py:455
  162.6 12.9 %collective-permute-start.54 = (bf16[8,48,128]{2,1,0:T(8,128)(2,1)S(1)}, bf16[8,48,128]{2,1,0:T(8,128)(2,1)S(1)}, u32[]{:S(2)}, u32[]{:S(2)}) collective-permute-start(bf16[8,48,128]{2,1,0:T(8,128)(2,1)S(1)} %get-tuple-element.29), channel_id=1, source_target_pairs={{0,28},{2,30},{4,24},{6,26},{8,20},{10,22},{12,16},{14,18},{16,12}... | collective-permute-start | bytes 294920 | tf_op jit(solution)/shard_map/ppermute | solution.py:455
  164.7 12.3 %collective-permute-start.55 = (bf16[8,48,128]{2,1,0:T(8,128)(2,1)S(1)}, bf16[8,48,128]{2,1,0:T(8,128)(2,1)S(1)}, u32[]{:S(2)}, u32[]{:S(2)}) collective-permute-start(bf16[8,48,128]{2,1,0:T(8,128)(2,1)S(1)} %get-tuple-element.28), channel_id=1, source_target_pairs={{0,4},{2,6},{4,0},{6,2},{8,12},{10,14},{12,8},{14,10},{16,20},{18,... | collective-permute-start | bytes 294920 | tf_op jit(solution)/shard_map/ppermute | solution.py:455
  167.2 21.0 %collective-permute-start.56 = (bf16[8,48,128]{2,1,0:T(8,128)(2,1)S(1)}, bf16[8,48,128]{2,1,0:T(8,128)(2,1)S(1)}, u32[]{:S(2)}, u32[]{:S(2)}) collective-permute-start(bf16[8,48,128]{2,1,0:T(8,128)(2,1)S(1)} %get-tuple-element.27), channel_id=1, source_target_pairs={{0,20},{2,22},{4,16},{6,18},{8,28},{10,30},{12,24},{14,26},{16,4},... | collective-permute-start | bytes 294920 | tf_op jit(solution)/shard_map/ppermute | solution.py:455
  172.2 18.4 %collective-permute-start.48 = (bf16[8,48,128]{2,1,0:T(8,128)(2,1)S(1)}, bf16[8,48,128]{2,1,0:T(8,128)(2,1)S(1)}, u32[]{:S(2)}, u32[]{:S(2)}) collective-permute-start(bf16[8,48,128]{2,1,0:T(8,128)(2,1)S(1)} %get-tuple-element.34), channel_id=1, source_target_pairs={{0,14},{2,12},{4,10},{6,8},{8,6},{10,4},{12,2},{14,0},{16,30},{18,... | collective-permute-start | bytes 294920 | tf_op jit(solution)/shard_map/ppermute | solution.py:455
  173.6 17.1 %collective-permute-start.49 = (bf16[8,48,128]{2,1,0:T(8,128)(2,1)S(1)}, bf16[8,48,128]{2,1,0:T(8,128)(2,1)S(1)}, u32[]{:S(2)}, u32[]{:S(2)}) collective-permute-start(bf16[8,48,128]{2,1,0:T(8,128)(2,1)S(1)} %get-tuple-element.33), channel_id=1, source_target_pairs={{0,30},{2,28},{4,26},{6,24},{8,22},{10,20},{12,18},{14,16},{16,14}... | collective-permute-start | bytes 294920 | tf_op jit(solution)/shard_map/ppermute | solution.py:455
  175.6 15.1 %collective-permute-start.50 = (bf16[8,48,128]{2,1,0:T(8,128)(2,1)S(1)}, bf16[8,48,128]{2,1,0:T(8,128)(2,1)S(1)}, u32[]{:S(2)}, u32[]{:S(2)}) collective-permute-start(bf16[8,48,128]{2,1,0:T(8,128)(2,1)S(1)} %get-tuple-element.32), channel_id=1, source_target_pairs={{0,6},{2,4},{4,2},{6,0},{8,14},{10,12},{12,10},{14,8},{16,22},{18,... | collective-permute-start | bytes 294920 | tf_op jit(solution)/shard_map/ppermute | solution.py:455
  177.0 13.6 %collective-permute-start.51 = (bf16[8,48,128]{2,1,0:T(8,128)(2,1)S(1)}, bf16[8,48,128]{2,1,0:T(8,128)(2,1)S(1)}, u32[]{:S(2)}, u32[]{:S(2)}) collective-permute-start(bf16[8,48,128]{2,1,0:T(8,128)(2,1)S(1)} %get-tuple-element.31), channel_id=1, source_target_pairs={{0,22},{2,20},{4,18},{6,16},{8,30},{10,28},{12,26},{14,24},{16,6},... | collective-permute-start | bytes 294920 | tf_op jit(solution)/shard_map/ppermute | solution.py:455
  (34 other events, 276.6 us)
where the time goes:
time: 195 us
  starting transfers between devices  127 us (65%)
  waiting for transfers between devices  34.7 us (18%)
  Pallas kernels  31.7 us (16%)
    ppermute x60, starting transfers between devices, local(): lax.ppermute(arrived[d], 'blk', [(g, g ^ d) for g in range(groups)])  122 us
    ppermute x60, waiting for transfers between devices, local(): lax.ppermute(arrived[d], 'blk', [(g, g ^ d) for g in range(groups)])  28.7 us
    pallas_call x3, Pallas kernels, leaf_stages(): pl.pallas_call(functools.partial(leaf_stage_kernel, groups, pairs, parts,...  10 us
    pallas_call x1, Pallas kernels, leaf_in(): pl.pallas_call(functools.partial(leaf_in_kernel, groups), out_shape=[jax....  6.8 us
    ppermute x4, waiting for transfers between devices, shared(): lax.ppermute(own, 'rhs', [(p, p ^ k) for p in range(parts)])  5.99 us
    pallas_call x6, Pallas kernels, mix_level(): pl.pallas_call(functools.partial(mix_early_kernel, groups, pairs), out_sh...  5.7 us
    ppermute x4, starting transfers between devices, shared(): lax.ppermute(own, 'rhs', [(p, p ^ k) for p in range(parts)])  4.95 us
    pallas_call x3, Pallas kernels, mix_level(): pl.pallas_call(functools.partial(mix_last_kernel, groups, stages[-1], sta...  4.49 us
  transfers between devices with their start and end apart: 64, of which 17 were waited for; matrix products, arithmetic and copies ran while one was open for 0% of the time, Pallas kernels for 11%

commit v1 on v0

--- a/solution.py
+++ b/solution.py
@@ -273,7 +273,8 @@
     mix_pairs(groups, pairs, blocks, weights, put)
 
 
-def mix_last_kernel(groups, pairs, early_pairs, target, slots_any, *refs):
+def mix_place_kernel(groups, pairs, early_pairs, onto, target, slots_any, *refs):
+    before, refs = (refs[0], refs[1:]) if onto else (None, refs)
     count = len(early_pairs)
     early, blocks = refs[:count], refs[count : count + 2 * len(pairs)]
     weights = refs[count + 2 * len(pairs) : -4]
@@ -287,6 +288,8 @@
         held[k, q] = value
 
     mix_pairs(groups, pairs, blocks, weights, put)
+    if onto:
+        out_ref[...] = before[...]
     copy.wait()
     for values, members in zip((*early, held), (*early_pairs, pairs)):
         for k, d in enumerate(e for d in members for e in (d, d ^ (groups // 2))):
@@ -377,7 +380,7 @@
     params = pltpu.CompilerParams(vmem_limit_bytes=12 * 2**20)
     used = [[blocks[d ^ h] for d in pairs for h in (0, groups // 2)] for pairs in stages]
     early = []
-    for k, pairs in enumerate(stages[:-1]):
+    for k, pairs in enumerate(stages[:-2]):
         early.append(
             pl.pallas_call(
                 functools.partial(mix_early_kernel, groups, pairs),
@@ -391,22 +394,29 @@
                 name="mix_early",
             )(*used[k], *weights)
         )
-    return pl.pallas_call(
-        functools.partial(
-            mix_last_kernel, groups, stages[-1], stages[:-1], level + 1
-        ),
-        out_shape=jax.ShapeDtypeStruct((groups * peer_blocks, rank, columns), jnp.bfloat16),
-        in_specs=[ANY] + [VMEM] * (len(early) + len(used[-1]) + parts),
-        out_specs=VMEM,
-        scratch_shapes=[
-            pltpu.VMEM((len(used[-1]), peer_blocks, rank, columns), jnp.bfloat16),
-            pltpu.SMEM(slots.shape, jnp.int32),
-            pltpu.SemaphoreType.DMA,
-        ],
-        compiler_params=params,
-        cost_estimate=cost(1),
-        name="mix_last",
-    )(slots, *early, *used[-1], *weights)
+    placed = None
+    for k in (len(stages) - 2, len(stages) - 1):
+        before = early if placed is None else [placed]
+        members = stages[:-2] if placed is None else ()
+        placed = pl.pallas_call(
+            functools.partial(
+                mix_place_kernel, groups, stages[k], members, placed is not None, level + 1
+            ),
+            out_shape=jax.ShapeDtypeStruct(
+                (groups * peer_blocks, rank, columns), jnp.bfloat16
+            ),
+            in_specs=[ANY] + [VMEM] * (len(before) + len(used[k]) + parts),
+            out_specs=VMEM,
+            scratch_shapes=[
+                pltpu.VMEM((len(used[k]), peer_blocks, rank, columns), jnp.bfloat16),
+                pltpu.SMEM(slots.shape, jnp.int32),
+                pltpu.SemaphoreType.DMA,
+            ],
+            compiler_params=params,
+            cost_estimate=cost(1),
+            name="mix_place",
+        )(slots, *before, *used[k], *weights)
+    return placed
 
 
 def stages_of(groups):

time: 195 us -> 194 us (level)
  starting transfers between devices: 127 us -> 122 us
  waiting for transfers between devices: 34.7 us -> 37.4 us
    ppermute x60, starting transfers between devices: 122 us -> 117 us  [local(): lax.ppermute(arrived[d], 'blk', [(g, g ^ d) for g in range(groups)])]
    pallas_call x3 -> x6, Pallas kernels: 4.49 us -> 8.06 us  [mix_level(): pl.pallas_call(functools.partial(mix_place_kernel, groups, stages[k], mem...]
    pallas_call x6 -> x3, Pallas kernels: 5.7 us -> 3.51 us  [mix_level(): pl.pallas_call(functools.partial(mix_early_kernel, groups, pairs), out_sh...]
  transfers between devices with their start and end apart: 64 -> 64, of which waited for: 17 -> 18; matrix products, arithmetic and copies ran while one was open for 0% -> 0% of each run, Pallas kernels for 11% -> 12%
where the time goes in v1:
time: 194 us
  starting transfers between devices  122 us (63%)
  waiting for transfers between devices  37.4 us (19%)
  Pallas kernels  33.1 us (17%)
    ppermute x60, starting transfers between devices, local(): lax.ppermute(arrived[d], 'blk', [(g, g ^ d) for g in range(groups)])  117 us
    ppermute x60, waiting for transfers between devices, local(): lax.ppermute(arrived[d], 'blk', [(g, g ^ d) for g in range(groups)])  30.4 us
    pallas_call x3, Pallas kernels, leaf_stages(): pl.pallas_call(functools.partial(leaf_stage_kernel, groups, pairs, parts,...  10 us
    pallas_call x6, Pallas kernels, mix_level(): pl.pallas_call(functools.partial(mix_place_kernel, groups, stages[k], mem...  8.06 us
    ppermute x4, waiting for transfers between devices, shared(): lax.ppermute(own, 'rhs', [(p, p ^ k) for p in range(parts)])  6.95 us
    pallas_call x1, Pallas kernels, leaf_in(): pl.pallas_call(functools.partial(leaf_in_kernel, groups), out_shape=[jax....  6.8 us
    ppermute x4, starting transfers between devices, shared(): lax.ppermute(own, 'rhs', [(p, p ^ k) for p in range(parts)])  4.94 us
  transfers between devices with their start and end apart: 64, of which 18 were waited for; matrix products, arithmetic and copies ran while one was open for 0% of the time, Pallas kernels for 12%

profile of v1, /device:TPU:1, one launch (start us, length us, event | category | flops | bytes accessed | tf_op | source)
XLA Modules:
  0.0 194.1 jit_solution(7882393538115337344)
XLA Ops:
  0.7 6.8 %leaf_in.1 = (bf16[128,48,128]{2,1,0:T(8,128)(2,1)S(1)}, s32[4,128]{1,0:T(4,128)S(1)}, bf16[1,2,32,48,192]{4,3,2,1,0:T(8,128)(2,1)S(1)}, bf16[96,48,128]{2,1,0:T(8,128)(2,1)S(1)}) custom-call(s32[5,128]{1,0:T(8,128)S(1)} %pad_add_fusion.leaves_ref, bf16[8192,128]{1,0:T(8,128)(2,1)} %signal_hbm.1, bf16[96,8192]{1,0:T(8,128)(2,1)} %factor_hbm.1, ...), custom_call_target="tpu_custom_call" | custom-call | flops 40000000 | tf_op jit(solution)/shard_map/leaf_in/pallas_call | solution.py:132
  16.1 4.0 %collective-permute-start.3 = (bf16[8,48,128]{2,1,0:T(8,128)(2,1)S(1)}, bf16[8,48,128]{2,1,0:T(8,128)(2,1)S(1)}, u32[]{:S(2)}, u32[]{:S(2)}) collective-permute-start(bf16[8,48,128]{2,1,0:T(8,128)(2,1)S(1)} %get-tuple-element.78), channel_id=1, source_target_pairs={{0,10},{2,8},{4,14},{6,12},{8,2},{10,0},{12,6},{14,4},{16,26},{18,... | collective-permute-start | bytes 294920 | tf_op jit(solution)/shard_map/ppermute | solution.py:465
  20.1 4.5 %collective-permute-start.4 = (bf16[8,48,128]{2,1,0:T(8,128)(2,1)S(1)}, bf16[8,48,128]{2,1,0:T(8,128)(2,1)S(1)}, u32[]{:S(2)}, u32[]{:S(2)}) collective-permute-start(bf16[8,48,128]{2,1,0:T(8,128)(2,1)S(1)} %get-tuple-element.77), channel_id=1, source_target_pairs={{0,26},{2,24},{4,30},{6,28},{8,18},{10,16},{12,22},{14,20},{16,10}... | collective-permute-start | bytes 294920 | tf_op jit(solution)/shard_map/ppermute | solution.py:465
  28.2 6.7 %collective-permute-start.11 = (bf16[8,48,128]{2,1,0:T(8,128)(2,1)S(1)}, bf16[8,48,128]{2,1,0:T(8,128)(2,1)S(1)}, u32[]{:S(2)}, u32[]{:S(2)}) collective-permute-start(bf16[8,48,128]{2,1,0:T(8,128)(2,1)S(1)} %get-tuple-element.71), channel_id=1, source_target_pairs={{0,20},{2,22},{4,16},{6,18},{8,28},{10,30},{12,24},{14,26},{16,4},... | collective-permute-start | bytes 294920 | tf_op jit(solution)/shard_map/ppermute | solution.py:465
  35.2 2.5 %collective-permute-start.9 = (bf16[8,48,128]{2,1,0:T(8,128)(2,1)S(1)}, bf16[8,48,128]{2,1,0:T(8,128)(2,1)S(1)}, u32[]{:S(2)}, u32[]{:S(2)}) collective-permute-start(bf16[8,48,128]{2,1,0:T(8,128)(2,1)S(1)} %get-tuple-element.73), channel_id=1, source_target_pairs={{0,28},{2,30},{4,24},{6,26},{8,20},{10,22},{12,16},{14,18},{16,12}... | collective-permute-start | bytes 294920 | tf_op jit(solution)/shard_map/ppermute | solution.py:465
  40.6 3.1 %collective-permute-start.13 = (bf16[8,48,128]{2,1,0:T(8,128)(2,1)S(1)}, bf16[8,48,128]{2,1,0:T(8,128)(2,1)S(1)}, u32[]{:S(2)}, u32[]{:S(2)}) collective-permute-start(bf16[8,48,128]{2,1,0:T(8,128)(2,1)S(1)} %get-tuple-element.69), channel_id=1, source_target_pairs={{0,30},{2,28},{4,26},{6,24},{8,22},{10,20},{12,18},{14,16},{16,14}... | collective-permute-start | bytes 294920 | tf_op jit(solution)/shard_map/ppermute | solution.py:465
  43.7 3.9 %collective-permute-start.14 = (bf16[8,48,128]{2,1,0:T(8,128)(2,1)S(1)}, bf16[8,48,128]{2,1,0:T(8,128)(2,1)S(1)}, u32[]{:S(2)}, u32[]{:S(2)}) collective-permute-start(bf16[8,48,128]{2,1,0:T(8,128)(2,1)S(1)} %get-tuple-element.68), channel_id=1, source_target_pairs={{0,6},{2,4},{4,2},{6,0},{8,14},{10,12},{12,10},{14,8},{16,22},{18,... | collective-permute-start | bytes 294920 | tf_op jit(solution)/shard_map/ppermute | solution.py:465
  47.7 5.5 %collective-permute-start.15 = (bf16[8,48,128]{2,1,0:T(8,128)(2,1)S(1)}, bf16[8,48,128]{2,1,0:T(8,128)(2,1)S(1)}, u32[]{:S(2)}, u32[]{:S(2)}) collective-permute-start(bf16[8,48,128]{2,1,0:T(8,128)(2,1)S(1)} %get-tuple-element.67), channel_id=1, source_target_pairs={{0,22},{2,20},{4,18},{6,16},{8,30},{10,28},{12,26},{14,24},{16,6},... | collective-permute-start | bytes 294920 | tf_op jit(solution)/shard_map/ppermute | solution.py:465
  59.4 2.5 %collective-permute-start.17 = (bf16[8,48,128]{2,1,0:T(8,128)(2,1)S(1)}, bf16[8,48,128]{2,1,0:T(8,128)(2,1)S(1)}, u32[]{:S(2)}, u32[]{:S(2)}) collective-permute-start(bf16[8,48,128]{2,1,0:T(8,128)(2,1)S(1)} %get-tuple-element.65), channel_id=1, source_target_pairs={{0,24},{2,26},{4,28},{6,30},{8,16},{10,18},{12,20},{14,22},{16,8},... | collective-permute-start | bytes 294920 | tf_op jit(solution)/shard_map/ppermute | solution.py:465
  62.0 6.9 %collective-permute-done.23.refs_9_.refs_6_ = bf16[1,2,32,48,192]{4,3,2,1,0:T(8,128)(2,1)S(1)} collective-permute-done((bf16[1,2,32,48,192]{4,3,2,1,0:T(8,128)(2,1)S(1)}, bf16[1,2,32,48,192]{4,3,2,1,0:T(8,128)(2,1)S(1)}, u32[]{:S(2)}, u32[]{:S(2)}) %collective-permute-start.23) | collective-permute-done | bytes 1179680 | tf_op jit(solution)/shard_map/ppermute | solution.py:451
  69.0 3.8 %collective-permute-start.19 = (bf16[8,48,128]{2,1,0:T(8,128)(2,1)S(1)}, bf16[8,48,128]{2,1,0:T(8,128)(2,1)S(1)}, u32[]{:S(2)}, u32[]{:S(2)}) collective-permute-start(bf16[8,48,128]{2,1,0:T(8,128)(2,1)S(1)} %get-tuple-element.62), channel_id=1, source_target_pairs={{0,10},{2,8},{4,14},{6,12},{8,2},{10,0},{12,6},{14,4},{16,26},{18,... | collective-permute-start | bytes 294920 | tf_op jit(solution)/shard_map/ppermute | solution.py:465
  77.7 2.7 %collective-permute-done.20.refs_5_ = bf16[8,48,128]{2,1,0:T(8,128)(2,1)S(1)} collective-permute-done((bf16[8,48,128]{2,1,0:T(8,128)(2,1)S(1)}, bf16[8,48,128]{2,1,0:T(8,128)(2,1)S(1)}, u32[]{:S(2)}, u32[]{:S(2)}) %collective-permute-start.20) | collective-permute-done | bytes 98336 | tf_op jit(solution)/shard_map/ppermute | solution.py:465
  80.4 2.6 %collective-permute-start.25 = (bf16[8,48,128]{2,1,0:T(8,128)(2,1)S(1)}, bf16[8,48,128]{2,1,0:T(8,128)(2,1)S(1)}, u32[]{:S(2)}, u32[]{:S(2)}) collective-permute-start(bf16[8,48,128]{2,1,0:T(8,128)(2,1)S(1)} %get-tuple-element.57), channel_id=1, source_target_pairs={{0,28},{2,30},{4,24},{6,26},{8,20},{10,22},{12,16},{14,18},{16,12}... | collective-permute-start | bytes 294920 | tf_op jit(solution)/shard_map/ppermute | solution.py:465
  87.0 4.7 %collective-permute-start.28 = (bf16[8,48,128]{2,1,0:T(8,128)(2,1)S(1)}, bf16[8,48,128]{2,1,0:T(8,128)(2,1)S(1)}, u32[]{:S(2)}, u32[]{:S(2)}) collective-permute-start(bf16[8,48,128]{2,1,0:T(8,128)(2,1)S(1)} %get-tuple-element.54), channel_id=1, source_target_pairs={{0,14},{2,12},{4,10},{6,8},{8,6},{10,4},{12,2},{14,0},{16,30},{18,... | collective-permute-start | bytes 294920 | tf_op jit(solution)/shard_map/ppermute | solution.py:465
  93.0 2.8 %collective-permute-start.30 = (bf16[8,48,128]{2,1,0:T(8,128)(2,1)S(1)}, bf16[8,48,128]{2,1,0:T(8,128)(2,1)S(1)}, u32[]{:S(2)}, u32[]{:S(2)}) collective-permute-start(bf16[8,48,128]{2,1,0:T(8,128)(2,1)S(1)} %get-tuple-element.52), channel_id=1, source_target_pairs={{0,6},{2,4},{4,2},{6,0},{8,14},{10,12},{12,10},{14,8},{16,22},{18,... | collective-permute-start | bytes 294920 | tf_op jit(solution)/shard_map/ppermute | solution.py:465
  95.8 4.6 %collective-permute-start.31 = (bf16[8,48,128]{2,1,0:T(8,128)(2,1)S(1)}, bf16[8,48,128]{2,1,0:T(8,128)(2,1)S(1)}, u32[]{:S(2)}, u32[]{:S(2)}) collective-permute-start(bf16[8,48,128]{2,1,0:T(8,128)(2,1)S(1)} %get-tuple-element.51), channel_id=1, source_target_pairs={{0,22},{2,20},{4,18},{6,16},{8,30},{10,28},{12,26},{14,24},{16,6},... | collective-permute-start | bytes 294920 | tf_op jit(solution)/shard_map/ppermute | solution.py:465
  103.0 3.1 %collective-permute-done.31.refs_4_ = bf16[8,48,128]{2,1,0:T(8,128)(2,1)S(1)} collective-permute-done((bf16[8,48,128]{2,1,0:T(8,128)(2,1)S(1)}, bf16[8,48,128]{2,1,0:T(8,128)(2,1)S(1)}, u32[]{:S(2)}, u32[]{:S(2)}) %collective-permute-start.31) | collective-permute-done | bytes 98336 | tf_op jit(solution)/shard_map/ppermute | solution.py:465
  110.3 2.5 %collective-permute-start.35 = (bf16[8,48,128]{2,1,0:T(8,128)(2,1)S(1)}, bf16[8,48,128]{2,1,0:T(8,128)(2,1)S(1)}, u32[]{:S(2)}, u32[]{:S(2)}) collective-permute-start(bf16[8,48,128]{2,1,0:T(8,128)(2,1)S(1)} %get-tuple-element.46), channel_id=1, source_target_pairs={{0,10},{2,8},{4,14},{6,12},{8,2},{10,0},{12,6},{14,4},{16,26},{18,... | collective-permute-start | bytes 294920 | tf_op jit(solution)/shard_map/ppermute | solution.py:465
  113.8 2.5 %collective-permute-start.37 = (bf16[8,48,128]{2,1,0:T(8,128)(2,1)S(1)}, bf16[8,48,128]{2,1,0:T(8,128)(2,1)S(1)}, u32[]{:S(2)}, u32[]{:S(2)}) collective-permute-start(bf16[8,48,128]{2,1,0:T(8,128)(2,1)S(1)} %get-tuple-element.44), channel_id=1, source_target_pairs={{0,2},{2,0},{4,6},{6,4},{8,10},{10,8},{12,14},{14,12},{16,18},{18,... | collective-permute-start | bytes 294920 | tf_op jit(solution)/shard_map/ppermute | solution.py:465
  116.4 3.4 %collective-permute-done.34.refs_3_ = bf16[8,48,128]{2,1,0:T(8,128)(2,1)S(1)} collective-permute-done((bf16[8,48,128]{2,1,0:T(8,128)(2,1)S(1)}, bf16[8,48,128]{2,1,0:T(8,128)(2,1)S(1)}, u32[]{:S(2)}, u32[]{:S(2)}) %collective-permute-start.34) | collective-permute-done | bytes 98336 | tf_op jit(solution)/shard_map/ppermute | solution.py:465
  119.8 2.9 %collective-permute-start.38 = (bf16[8,48,128]{2,1,0:T(8,128)(2,1)S(1)}, bf16[8,48,128]{2,1,0:T(8,128)(2,1)S(1)}, u32[]{:S(2)}, u32[]{:S(2)}) collective-permute-start(bf16[8,48,128]{2,1,0:T(8,128)(2,1)S(1)} %get-tuple-element.43), channel_id=1, source_target_pairs={{0,18},{2,16},{4,22},{6,20},{8,26},{10,24},{12,30},{14,28},{16,2},... | collective-permute-start | bytes 294920 | tf_op jit(solution)/shard_map/ppermute | solution.py:465
  122.7 3.0 %collective-permute-start.40 = (bf16[8,48,128]{2,1,0:T(8,128)(2,1)S(1)}, bf16[8,48,128]{2,1,0:T(8,128)(2,1)S(1)}, u32[]{:S(2)}, u32[]{:S(2)}) collective-permute-start(bf16[8,48,128]{2,1,0:T(8,128)(2,1)S(1)} %get-tuple-element.42), channel_id=1, source_target_pairs={{0,12},{2,14},{4,8},{6,10},{8,4},{10,6},{12,0},{14,2},{16,28},{18,... | collective-permute-start | bytes 294920 | tf_op jit(solution)/shard_map/ppermute | solution.py:465
  133.8 6.4 %collective-permute-done.42.refs_3_ = bf16[8,48,128]{2,1,0:T(8,128)(2,1)S(1)} collective-permute-done((bf16[8,48,128]{2,1,0:T(8,128)(2,1)S(1)}, bf16[8,48,128]{2,1,0:T(8,128)(2,1)S(1)}, u32[]{:S(2)}, u32[]{:S(2)}) %collective-permute-start.42) | collective-permute-done | bytes 98336 | tf_op jit(solution)/shard_map/ppermute | solution.py:465
  145.3 2.6 %collective-permute-done.47.refs_4_ = bf16[8,48,128]{2,1,0:T(8,128)(2,1)S(1)} collective-permute-done((bf16[8,48,128]{2,1,0:T(8,128)(2,1)S(1)}, bf16[8,48,128]{2,1,0:T(8,128)(2,1)S(1)}, u32[]{:S(2)}, u32[]{:S(2)}) %collective-permute-start.47) | collective-permute-done | bytes 98336 | tf_op jit(solution)/shard_map/ppermute | solution.py:465
  156.0 5.1 %collective-permute-start.63 = (bf16[8,48,128]{2,1,0:T(8,128)(2,1)S(1)}, bf16[8,48,128]{2,1,0:T(8,128)(2,1)S(1)}, u32[]{:S(2)}, u32[]{:S(2)}) collective-permute-start(bf16[8,48,128]{2,1,0:T(8,128)(2,1)S(1)} %get-tuple-element.19), channel_id=1, source_target_pairs={{0,18},{2,16},{4,22},{6,20},{8,26},{10,24},{12,30},{14,28},{16,2},... | collective-permute-start | bytes 294920 | tf_op jit(solution)/shard_map/ppermute | solution.py:465
  161.1 3.0 %collective-permute-done.59.refs_3_ = bf16[8,48,128]{2,1,0:T(8,128)(2,1)S(1)} collective-permute-done((bf16[8,48,128]{2,1,0:T(8,128)(2,1)S(1)}, bf16[8,48,128]{2,1,0:T(8,128)(2,1)S(1)}, u32[]{:S(2)}, u32[]{:S(2)}) %collective-permute-start.59) | collective-permute-done | bytes 98336 | tf_op jit(solution)/shard_map/ppermute | solution.py:465
  166.4 5.1 %collective-permute-start.56 = (bf16[8,48,128]{2,1,0:T(8,128)(2,1)S(1)}, bf16[8,48,128]{2,1,0:T(8,128)(2,1)S(1)}, u32[]{:S(2)}, u32[]{:S(2)}) collective-permute-start(bf16[8,48,128]{2,1,0:T(8,128)(2,1)S(1)} %get-tuple-element.27), channel_id=1, source_target_pairs={{0,20},{2,22},{4,16},{6,18},{8,28},{10,30},{12,24},{14,26},{16,4},... | collective-permute-start | bytes 294920 | tf_op jit(solution)/shard_map/ppermute | solution.py:465
  172.4 3.1 %collective-permute-start.49 = (bf16[8,48,128]{2,1,0:T(8,128)(2,1)S(1)}, bf16[8,48,128]{2,1,0:T(8,128)(2,1)S(1)}, u32[]{:S(2)}, u32[]{:S(2)}) collective-permute-start(bf16[8,48,128]{2,1,0:T(8,128)(2,1)S(1)} %get-tuple-element.33), channel_id=1, source_target_pairs={{0,30},{2,28},{4,26},{6,24},{8,22},{10,20},{12,18},{14,16},{16,14}... | collective-permute-start | bytes 294920 | tf_op jit(solution)/shard_map/ppermute | solution.py:465
  176.3 5.8 %collective-permute-start.51 = (bf16[8,48,128]{2,1,0:T(8,128)(2,1)S(1)}, bf16[8,48,128]{2,1,0:T(8,128)(2,1)S(1)}, u32[]{:S(2)}, u32[]{:S(2)}) collective-permute-start(bf16[8,48,128]{2,1,0:T(8,128)(2,1)S(1)} %get-tuple-element.31), channel_id=1, source_target_pairs={{0,22},{2,20},{4,18},{6,16},{8,30},{10,28},{12,26},{14,24},{16,6},... | collective-permute-start | bytes 294920 | tf_op jit(solution)/shard_map/ppermute | solution.py:465
  183.8 3.8 %leaf_stage.3.refs_6_ = bf16[8336,128]{1,0:T(8,128)(2,1)S(1)} custom-call(s32[1,128]{1,0:T(1,128)S(1)} %copy-done.1, bf16[8336,128]{1,0:T(8,128)(2,1)S(1)} %flip.1.factor, bf16[8,48,128]{2,1,0:T(8,128)(2,1)S(1)} %collective-permute-done.57.refs_0_, bf16[8,48,128]{2,1,0:T(8,128)(2,1)S(1)} %collective-permute-done.58.refs_1_, ...), custom_call_target="tpu_custom_call" | custom-call | flops 20000000 | tf_op jit(solution)/shard_map/leaf_stage/pallas_call | solution.py:356
  187.6 2.4 %leaf_stage.4.refs_6_ = bf16[8336,128]{1,0:T(8,128)(2,1)S(1)} custom-call(s32[1,128]{1,0:T(1,128)S(1)} %copy-done.1, bf16[8336,128]{1,0:T(8,128)(2,1)S(1)} %flip.1.factor, bf16[8,48,128]{2,1,0:T(8,128)(2,1)S(1)} %collective-permute-done.53.refs_0_, bf16[8,48,128]{2,1,0:T(8,128)(2,1)S(1)} %collective-permute-done.54.refs_1_, ...), custom_call_target="tpu_custom_call" | custom-call | flops 20000000 | tf_op jit(solution)/shard_map/leaf_stage/pallas_call | solution.py:356
  190.1 3.8 %leaf_stage.5 = bf16[8192,128]{1,0:T(8,128)(2,1)} custom-call(s32[1,128]{1,0:T(1,128)S(1)} %copy-done.1, bf16[8336,128]{1,0:T(8,128)(2,1)S(1)} %flip.1.factor, bf16[8,48,128]{2,1,0:T(8,128)(2,1)S(1)} %collective-permute-done.48.refs_0_, bf16[8,48,128]{2,1,0:T(8,128)(2,1)S(1)} %collective-permute-done.49.refs_1_, ...), custom_call_target="tpu_custom_call" | custom-call | flops 20000000 | tf_op jit(solution)/shard_map/leaf_stage/pallas_call | solution.py:356
  (121 shorter events, 67.3 us)
Async XLA Ops:
  7.5 45.6 %collective-permute-start.7 = (bf16[96,48,128]{2,1,0:T(8,128)(2,1)S(1)}, bf16[96,48,128]{2,1,0:T(8,128)(2,1)S(1)}, u32[]{:S(2)}, u32[]{:S(2)}) collective-permute-start(bf16[96,48,128]{2,1,0:T(8,128)(2,1)S(1)} %get-tuple-element.15), channel_id=1, source_target_pairs={{0,1},{1,0},{2,3},{3,2},{4,5},{5,4},{6,7},{7,6},{8,9},{9,8},{10,11... | collective-permute-start | bytes 3538952 | tf_op jit(solution)/shard_map/ppermute | solution.py:451
  12.0 57.0 %collective-permute-start.23 = (bf16[1,2,32,48,192]{4,3,2,1,0:T(8,128)(2,1)S(1)}, bf16[1,2,32,48,192]{4,3,2,1,0:T(8,128)(2,1)S(1)}, u32[]{:S(2)}, u32[]{:S(2)}) collective-permute-start(bf16[1,2,32,48,192]{4,3,2,1,0:T(8,128)(2,1)S(1)} %get-tuple-element.16.refs_8_.refs_5_), channel_id=1, source_target_pairs={{0,1},{1,0},{2,3},{3,2},{4,5},{5,4},{6,7},{7,6},{8,9},{9,8},{10,11... | collective-permute-start | bytes 3538952 | tf_op jit(solution)/shard_map/ppermute | solution.py:451
  28.2 11.1 %collective-permute-start.11 = (bf16[8,48,128]{2,1,0:T(8,128)(2,1)S(1)}, bf16[8,48,128]{2,1,0:T(8,128)(2,1)S(1)}, u32[]{:S(2)}, u32[]{:S(2)}) collective-permute-start(bf16[8,48,128]{2,1,0:T(8,128)(2,1)S(1)} %get-tuple-element.71), channel_id=1, source_target_pairs={{0,20},{2,22},{4,16},{6,18},{8,28},{10,30},{12,24},{14,26},{16,4},... | collective-permute-start | bytes 294920 | tf_op jit(solution)/shard_map/ppermute | solution.py:465
  40.6 17.3 %collective-permute-start.13 = (bf16[8,48,128]{2,1,0:T(8,128)(2,1)S(1)}, bf16[8,48,128]{2,1,0:T(8,128)(2,1)S(1)}, u32[]{:S(2)}, u32[]{:S(2)}) collective-permute-start(bf16[8,48,128]{2,1,0:T(8,128)(2,1)S(1)} %get-tuple-element.69), channel_id=1, source_target_pairs={{0,30},{2,28},{4,26},{6,24},{8,22},{10,20},{12,18},{14,16},{16,14}... | collective-permute-start | bytes 294920 | tf_op jit(solution)/shard_map/ppermute | solution.py:465
  43.7 14.2 %collective-permute-start.14 = (bf16[8,48,128]{2,1,0:T(8,128)(2,1)S(1)}, bf16[8,48,128]{2,1,0:T(8,128)(2,1)S(1)}, u32[]{:S(2)}, u32[]{:S(2)}) collective-permute-start(bf16[8,48,128]{2,1,0:T(8,128)(2,1)S(1)} %get-tuple-element.68), channel_id=1, source_target_pairs={{0,6},{2,4},{4,2},{6,0},{8,14},{10,12},{12,10},{14,8},{16,22},{18,... | collective-permute-start | bytes 294920 | tf_op jit(solution)/shard_map/ppermute | solution.py:465
  53.1 57.2 %collective-permute-start.39 = (bf16[1,2,32,48,192]{4,3,2,1,0:T(8,128)(2,1)S(1)}, bf16[1,2,32,48,192]{4,3,2,1,0:T(8,128)(2,1)S(1)}, u32[]{:S(2)}, u32[]{:S(2)}) collective-permute-start(bf16[1,2,32,48,192]{4,3,2,1,0:T(8,128)(2,1)S(1)} %get-tuple-element.17.refs_8_.refs_5_), channel_id=1, source_target_pairs={{0,1},{1,0},{2,3},{3,2},{4,5},{5,4},{6,7},{7,6},{8,9},{9,8},{10,11... | collective-permute-start | bytes 3538952 | tf_op jit(solution)/shard_map/ppermute | solution.py:451
  59.3 13.5 %collective-permute-start.16 = (bf16[8,48,128]{2,1,0:T(8,128)(2,1)S(1)}, bf16[8,48,128]{2,1,0:T(8,128)(2,1)S(1)}, u32[]{:S(2)}, u32[]{:S(2)}) collective-permute-start(bf16[8,48,128]{2,1,0:T(8,128)(2,1)S(1)} %get-tuple-element.66), channel_id=1, source_target_pairs={{0,8},{2,10},{4,12},{6,14},{8,0},{10,2},{12,4},{14,6},{16,24},{18,... | collective-permute-start | bytes 294920 | tf_op jit(solution)/shard_map/ppermute | solution.py:465
  59.4 15.4 %collective-permute-start.17 = (bf16[8,48,128]{2,1,0:T(8,128)(2,1)S(1)}, bf16[8,48,128]{2,1,0:T(8,128)(2,1)S(1)}, u32[]{:S(2)}, u32[]{:S(2)}) collective-permute-start(bf16[8,48,128]{2,1,0:T(8,128)(2,1)S(1)} %get-tuple-element.65), channel_id=1, source_target_pairs={{0,24},{2,26},{4,28},{6,30},{8,16},{10,18},{12,20},{14,22},{16,8},... | collective-permute-start | bytes 294920 | tf_op jit(solution)/shard_map/ppermute | solution.py:465
  61.9 13.5 %collective-permute-start.18 = (bf16[8,48,128]{2,1,0:T(8,128)(2,1)S(1)}, bf16[8,48,128]{2,1,0:T(8,128)(2,1)S(1)}, u32[]{:S(2)}, u32[]{:S(2)}) collective-permute-start(bf16[8,48,128]{2,1,0:T(8,128)(2,1)S(1)} %get-tuple-element.63), channel_id=1, source_target_pairs={{0,16},{2,18},{4,20},{6,22},{8,24},{10,26},{12,28},{14,30},{16,0},... | collective-permute-start | bytes 294920 | tf_op jit(solution)/shard_map/ppermute | solution.py:465
  83.0 70.9 %collective-permute-start.52 = (bf16[1,2,32,48,192]{4,3,2,1,0:T(8,128)(2,1)S(1)}, bf16[1,2,32,48,192]{4,3,2,1,0:T(8,128)(2,1)S(1)}, u32[]{:S(2)}, u32[]{:S(2)}) collective-permute-start(bf16[1,2,32,48,192]{4,3,2,1,0:T(8,128)(2,1)S(1)} %get-tuple-element.18.refs_8_.refs_4_), channel_id=1, source_target_pairs={{0,1},{1,0},{2,3},{3,2},{4,5},{5,4},{6,7},{7,6},{8,9},{9,8},{10,11... | collective-permute-start | bytes 3538952 | tf_op jit(solution)/shard_map/ppermute | solution.py:451
  91.7 11.4 %collective-permute-start.29 = (bf16[8,48,128]{2,1,0:T(8,128)(2,1)S(1)}, bf16[8,48,128]{2,1,0:T(8,128)(2,1)S(1)}, u32[]{:S(2)}, u32[]{:S(2)}) collective-permute-start(bf16[8,48,128]{2,1,0:T(8,128)(2,1)S(1)} %get-tuple-element.53), channel_id=1, source_target_pairs={{0,30},{2,28},{4,26},{6,24},{8,22},{10,20},{12,18},{14,16},{16,14}... | collective-permute-start | bytes 294920 | tf_op jit(solution)/shard_map/ppermute | solution.py:465
  95.8 10.4 %collective-permute-start.31 = (bf16[8,48,128]{2,1,0:T(8,128)(2,1)S(1)}, bf16[8,48,128]{2,1,0:T(8,128)(2,1)S(1)}, u32[]{:S(2)}, u32[]{:S(2)}) collective-permute-start(bf16[8,48,128]{2,1,0:T(8,128)(2,1)S(1)} %get-tuple-element.51), channel_id=1, source_target_pairs={{0,22},{2,20},{4,18},{6,16},{8,30},{10,28},{12,26},{14,24},{16,6},... | collective-permute-start | bytes 294920 | tf_op jit(solution)/shard_map/ppermute | solution.py:465
  108.4 11.3 %collective-permute-start.34 = (bf16[8,48,128]{2,1,0:T(8,128)(2,1)S(1)}, bf16[8,48,128]{2,1,0:T(8,128)(2,1)S(1)}, u32[]{:S(2)}, u32[]{:S(2)}) collective-permute-start(bf16[8,48,128]{2,1,0:T(8,128)(2,1)S(1)} %get-tuple-element.47), channel_id=1, source_target_pairs={{0,16},{2,18},{4,20},{6,22},{8,24},{10,26},{12,28},{14,30},{16,0},... | collective-permute-start | bytes 294920 | tf_op jit(solution)/shard_map/ppermute | solution.py:465
  110.3 12.4 %collective-permute-start.35 = (bf16[8,48,128]{2,1,0:T(8,128)(2,1)S(1)}, bf16[8,48,128]{2,1,0:T(8,128)(2,1)S(1)}, u32[]{:S(2)}, u32[]{:S(2)}) collective-permute-start(bf16[8,48,128]{2,1,0:T(8,128)(2,1)S(1)} %get-tuple-element.46), channel_id=1, source_target_pairs={{0,10},{2,8},{4,14},{6,12},{8,2},{10,0},{12,6},{14,4},{16,26},{18,... | collective-permute-start | bytes 294920 | tf_op jit(solution)/shard_map/ppermute | solution.py:465
  112.8 12.8 %collective-permute-start.36 = (bf16[8,48,128]{2,1,0:T(8,128)(2,1)S(1)}, bf16[8,48,128]{2,1,0:T(8,128)(2,1)S(1)}, u32[]{:S(2)}, u32[]{:S(2)}) collective-permute-start(bf16[8,48,128]{2,1,0:T(8,128)(2,1)S(1)} %get-tuple-element.45), channel_id=1, source_target_pairs={{0,26},{2,24},{4,30},{6,28},{8,18},{10,16},{12,22},{14,20},{16,10}... | collective-permute-start | bytes 294920 | tf_op jit(solution)/shard_map/ppermute | solution.py:465
  113.8 14.0 %collective-permute-start.37 = (bf16[8,48,128]{2,1,0:T(8,128)(2,1)S(1)}, bf16[8,48,128]{2,1,0:T(8,128)(2,1)S(1)}, u32[]{:S(2)}, u32[]{:S(2)}) collective-permute-start(bf16[8,48,128]{2,1,0:T(8,128)(2,1)S(1)} %get-tuple-element.44), channel_id=1, source_target_pairs={{0,2},{2,0},{4,6},{6,4},{8,10},{10,8},{12,14},{14,12},{16,18},{18,... | collective-permute-start | bytes 294920 | tf_op jit(solution)/shard_map/ppermute | solution.py:465
  127.9 12.3 %collective-permute-start.42 = (bf16[8,48,128]{2,1,0:T(8,128)(2,1)S(1)}, bf16[8,48,128]{2,1,0:T(8,128)(2,1)S(1)}, u32[]{:S(2)}, u32[]{:S(2)}) collective-permute-start(bf16[8,48,128]{2,1,0:T(8,128)(2,1)S(1)} %get-tuple-element.40), channel_id=1, source_target_pairs={{0,4},{2,6},{4,0},{6,2},{8,12},{10,14},{12,8},{14,10},{16,20},{18,... | collective-permute-start | bytes 294920 | tf_op jit(solution)/shard_map/ppermute | solution.py:465
  127.9 12.3 %collective-permute-start.43 = (bf16[8,48,128]{2,1,0:T(8,128)(2,1)S(1)}, bf16[8,48,128]{2,1,0:T(8,128)(2,1)S(1)}, u32[]{:S(2)}, u32[]{:S(2)}) collective-permute-start(bf16[8,48,128]{2,1,0:T(8,128)(2,1)S(1)} %get-tuple-element.39), channel_id=1, source_target_pairs={{0,20},{2,22},{4,16},{6,18},{8,28},{10,30},{12,24},{14,26},{16,4},... | collective-permute-start | bytes 294920 | tf_op jit(solution)/shard_map/ppermute | solution.py:465
  129.4 13.5 %collective-permute-start.44 = (bf16[8,48,128]{2,1,0:T(8,128)(2,1)S(1)}, bf16[8,48,128]{2,1,0:T(8,128)(2,1)S(1)}, u32[]{:S(2)}, u32[]{:S(2)}) collective-permute-start(bf16[8,48,128]{2,1,0:T(8,128)(2,1)S(1)} %get-tuple-element.38), channel_id=1, source_target_pairs={{0,14},{2,12},{4,10},{6,8},{8,6},{10,4},{12,2},{14,0},{16,30},{18,... | collective-permute-start | bytes 294920 | tf_op jit(solution)/shard_map/ppermute | solution.py:465
  132.1 10.8 %collective-permute-start.45 = (bf16[8,48,128]{2,1,0:T(8,128)(2,1)S(1)}, bf16[8,48,128]{2,1,0:T(8,128)(2,1)S(1)}, u32[]{:S(2)}, u32[]{:S(2)}) collective-permute-start(bf16[8,48,128]{2,1,0:T(8,128)(2,1)S(1)} %get-tuple-element.37), channel_id=1, source_target_pairs={{0,30},{2,28},{4,26},{6,24},{8,22},{10,20},{12,18},{14,16},{16,14}... | collective-permute-start | bytes 294920 | tf_op jit(solution)/shard_map/ppermute | solution.py:465
  149.9 14.2 %collective-permute-start.59 = (bf16[8,48,128]{2,1,0:T(8,128)(2,1)S(1)}, bf16[8,48,128]{2,1,0:T(8,128)(2,1)S(1)}, u32[]{:S(2)}, u32[]{:S(2)}) collective-permute-start(bf16[8,48,128]{2,1,0:T(8,128)(2,1)S(1)} %get-tuple-element.23), channel_id=1, source_target_pairs={{0,16},{2,18},{4,20},{6,22},{8,24},{10,26},{12,28},{14,30},{16,0},... | collective-permute-start | bytes 294920 | tf_op jit(solution)/shard_map/ppermute | solution.py:465
  152.0 12.0 %collective-permute-start.60 = (bf16[8,48,128]{2,1,0:T(8,128)(2,1)S(1)}, bf16[8,48,128]{2,1,0:T(8,128)(2,1)S(1)}, u32[]{:S(2)}, u32[]{:S(2)}) collective-permute-start(bf16[8,48,128]{2,1,0:T(8,128)(2,1)S(1)} %get-tuple-element.22), channel_id=1, source_target_pairs={{0,10},{2,8},{4,14},{6,12},{8,2},{10,0},{12,6},{14,4},{16,26},{18,... | collective-permute-start | bytes 294920 | tf_op jit(solution)/shard_map/ppermute | solution.py:465
  153.8 10.4 %collective-permute-start.61 = (bf16[8,48,128]{2,1,0:T(8,128)(2,1)S(1)}, bf16[8,48,128]{2,1,0:T(8,128)(2,1)S(1)}, u32[]{:S(2)}, u32[]{:S(2)}) collective-permute-start(bf16[8,48,128]{2,1,0:T(8,128)(2,1)S(1)} %get-tuple-element.21), channel_id=1, source_target_pairs={{0,26},{2,24},{4,30},{6,28},{8,18},{10,16},{12,22},{14,20},{16,10}... | collective-permute-start | bytes 294920 | tf_op jit(solution)/shard_map/ppermute | solution.py:465
  154.6 11.8 %collective-permute-start.62 = (bf16[8,48,128]{2,1,0:T(8,128)(2,1)S(1)}, bf16[8,48,128]{2,1,0:T(8,128)(2,1)S(1)}, u32[]{:S(2)}, u32[]{:S(2)}) collective-permute-start(bf16[8,48,128]{2,1,0:T(8,128)(2,1)S(1)} %get-tuple-element.20), channel_id=1, source_target_pairs={{0,2},{2,0},{4,6},{6,4},{8,10},{10,8},{12,14},{14,12},{16,18},{18,... | collective-permute-start | bytes 294920 | tf_op jit(solution)/shard_map/ppermute | solution.py:465
  156.0 16.0 %collective-permute-start.63 = (bf16[8,48,128]{2,1,0:T(8,128)(2,1)S(1)}, bf16[8,48,128]{2,1,0:T(8,128)(2,1)S(1)}, u32[]{:S(2)}, u32[]{:S(2)}) collective-permute-start(bf16[8,48,128]{2,1,0:T(8,128)(2,1)S(1)} %get-tuple-element.19), channel_id=1, source_target_pairs={{0,18},{2,16},{4,22},{6,20},{8,26},{10,24},{12,30},{14,28},{16,2},... | collective-permute-start | bytes 294920 | tf_op jit(solution)/shard_map/ppermute | solution.py:465
  164.1 11.5 %collective-permute-start.54 = (bf16[8,48,128]{2,1,0:T(8,128)(2,1)S(1)}, bf16[8,48,128]{2,1,0:T(8,128)(2,1)S(1)}, u32[]{:S(2)}, u32[]{:S(2)}) collective-permute-start(bf16[8,48,128]{2,1,0:T(8,128)(2,1)S(1)} %get-tuple-element.29), channel_id=1, source_target_pairs={{0,28},{2,30},{4,24},{6,26},{8,20},{10,22},{12,16},{14,18},{16,12}... | collective-permute-start | bytes 294920 | tf_op jit(solution)/shard_map/ppermute | solution.py:465
  164.2 12.1 %collective-permute-start.55 = (bf16[8,48,128]{2,1,0:T(8,128)(2,1)S(1)}, bf16[8,48,128]{2,1,0:T(8,128)(2,1)S(1)}, u32[]{:S(2)}, u32[]{:S(2)}) collective-permute-start(bf16[8,48,128]{2,1,0:T(8,128)(2,1)S(1)} %get-tuple-element.28), channel_id=1, source_target_pairs={{0,4},{2,6},{4,0},{6,2},{8,12},{10,14},{12,8},{14,10},{16,20},{18,... | collective-permute-start | bytes 294920 | tf_op jit(solution)/shard_map/ppermute | solution.py:465
  166.4 21.2 %collective-permute-start.56 = (bf16[8,48,128]{2,1,0:T(8,128)(2,1)S(1)}, bf16[8,48,128]{2,1,0:T(8,128)(2,1)S(1)}, u32[]{:S(2)}, u32[]{:S(2)}) collective-permute-start(bf16[8,48,128]{2,1,0:T(8,128)(2,1)S(1)} %get-tuple-element.27), channel_id=1, source_target_pairs={{0,20},{2,22},{4,16},{6,18},{8,28},{10,30},{12,24},{14,26},{16,4},... | collective-permute-start | bytes 294920 | tf_op jit(solution)/shard_map/ppermute | solution.py:465
  172.0 18.1 %collective-permute-start.48 = (bf16[8,48,128]{2,1,0:T(8,128)(2,1)S(1)}, bf16[8,48,128]{2,1,0:T(8,128)(2,1)S(1)}, u32[]{:S(2)}, u32[]{:S(2)}) collective-permute-start(bf16[8,48,128]{2,1,0:T(8,128)(2,1)S(1)} %get-tuple-element.34), channel_id=1, source_target_pairs={{0,14},{2,12},{4,10},{6,8},{8,6},{10,4},{12,2},{14,0},{16,30},{18,... | collective-permute-start | bytes 294920 | tf_op jit(solution)/shard_map/ppermute | solution.py:465
  172.4 17.7 %collective-permute-start.49 = (bf16[8,48,128]{2,1,0:T(8,128)(2,1)S(1)}, bf16[8,48,128]{2,1,0:T(8,128)(2,1)S(1)}, u32[]{:S(2)}, u32[]{:S(2)}) collective-permute-start(bf16[8,48,128]{2,1,0:T(8,128)(2,1)S(1)} %get-tuple-element.33), channel_id=1, source_target_pairs={{0,30},{2,28},{4,26},{6,24},{8,22},{10,20},{12,18},{14,16},{16,14}... | collective-permute-start | bytes 294920 | tf_op jit(solution)/shard_map/ppermute | solution.py:465
  175.6 14.5 %collective-permute-start.50 = (bf16[8,48,128]{2,1,0:T(8,128)(2,1)S(1)}, bf16[8,48,128]{2,1,0:T(8,128)(2,1)S(1)}, u32[]{:S(2)}, u32[]{:S(2)}) collective-permute-start(bf16[8,48,128]{2,1,0:T(8,128)(2,1)S(1)} %get-tuple-element.32), channel_id=1, source_target_pairs={{0,6},{2,4},{4,2},{6,0},{8,14},{10,12},{12,10},{14,8},{16,22},{18,... | collective-permute-start | bytes 294920 | tf_op jit(solution)/shard_map/ppermute | solution.py:465
  176.3 13.8 %collective-permute-start.51 = (bf16[8,48,128]{2,1,0:T(8,128)(2,1)S(1)}, bf16[8,48,128]{2,1,0:T(8,128)(2,1)S(1)}, u32[]{:S(2)}, u32[]{:S(2)}) collective-permute-start(bf16[8,48,128]{2,1,0:T(8,128)(2,1)S(1)} %get-tuple-element.31), channel_id=1, source_target_pairs={{0,22},{2,20},{4,18},{6,16},{8,30},{10,28},{12,26},{14,24},{16,6},... | collective-permute-start | bytes 294920 | tf_op jit(solution)/shard_map/ppermute | solution.py:465
  (34 other events, 276.0 us)
